TPU v7x, 1024 devices: a whole 4x4x32 slice. The times are simulated.
1024 devices in a mesh: gx: 8 (over z_hi, core), gy: 4 (over x), gz: 32 (over z_lo, y).
Axes of the slice: x: 4, y: 4, z: 32 (z_hi: 4, z_lo: 8; z = z_hi * 8 + z_lo), core: 2. Of those that a mesh axis runs over, the one named last changes fastest.
Arguments:
- euler_state: float32 [5, 32, 32, 4096], P(None, 'gx', 'gy', 'gz'), as said below
- gravity_state: float32 [4, 32, 32, 4096], P(None, 'gx', 'gy', 'gz'), may hold values from -6 to 6
Outputs:
- section_rate: float32 [5, 32, 32, 4096], P(None, 'gx', 'gy', 'gz')
- gravity_next: float32 [4, 32, 32, 4096], P(None, 'gx', 'gy', 'gz')
- gravity_source: float32 [4, 32, 32, 4096], P(None, 'gx', 'gy', 'gz')
- residual_norm: float32 [], replicated
Inputs may be any that keep to these rules, and one draw needn't show every extreme that they name: `euler_state`: each node's density lies between 0.7 and 3.9 and its pressure, for a ratio of specific heats of 1.4, between 0.7 and 71.
All inputs are finite; a program needn't handle non-finite values.
Results may differ from a plain program's by a relative error of at most 0.0003.
Values sent between devices are 32-bit elements; how exact they have to be, the bound alone decides.
No kernel may reach another device: no remote copies, remote signals or barrier semaphores. Data moves between devices by JAX's collectives and lax.ppermute only.
A program may use at most 32 MiB of HBM per device.

v0:
```python
import functools
import math

import jax
import jax.numpy as jnp
import numpy as np
from jax import lax
from jax.sharding import Mesh
from jax.sharding import PartitionSpec as P

ITERS = 3
GX_GY_GZ = ("gx_0", "gx_1", "gy", "gz_0", "gz_1")
GX = ("gx_0", "gx_1")
GZ = ("gz_0", "gz_1")


gamma_gas = 1.4
elem_width = 1.0
cfl_euler = 0.5
alpha_most = 0.5
indicator_level = 0.5 * 10.0 ** (-1.8 * 4.0**0.25)
indicator_slope = math.log((1.0 - 0.0001) / 0.0001) / indicator_level
coupling = 10.0
relax_time = 1.0
grav_speed = 1.0
pseudo_step = 0.3 * elem_width / 7.0


def with_halo(value, sides, width):
    edges = {}
    for axis, dim in sides:
        size, length = (lax.axis_size(axis), value.shape[dim])
        up = [(i, (i + 1) % size) for i in range(size)]
        last = lax.slice_in_dim(value, length - width, length, axis=dim)
        first = lax.slice_in_dim(value, 0, width, axis=dim)
        edges[dim] = (
            lax.ppermute(last, axis, up),
            lax.ppermute(first, axis, [(b, a) for a, b in up]),
        )
    done = []
    for _, dim in sides:
        low, high = edges[dim]
        around = [(width, width) if d in done else (0, 0) for d in range(value.ndim)]
        value = jnp.concatenate([jnp.pad(low, around), value, jnp.pad(high, around)], axis=dim)
        done.append(dim)
    return value


def by_axis(value, axes):
    return functools.reduce(lax.psum, axes, value)


def over_axes(value, axes):
    for axis in axes:
        value = lax.pmax(value, axis)
    return value


def lgl_tables():
    points = np.array([-1.0, -1.0 / math.sqrt(5.0), 1.0 / math.sqrt(5.0), 1.0])
    weights = np.array([1.0, 5.0, 5.0, 1.0]) / 6.0
    barycentric = np.array(
        [
            1.0
            / np.prod([points[node_a] - points[node_b] for node_b in range(4) if node_b != node_a])
            for node_a in range(4)
        ]
    )
    derivative = np.zeros((4, 4))
    for node_a in range(4):
        for node_b in range(4):
            if node_b != node_a:
                derivative[node_a, node_b] = (
                    barycentric[node_b] / barycentric[node_a] / (points[node_a] - points[node_b])
                )
        derivative[node_a, node_a] = -np.sum(derivative[node_a])
    legendre = np.stack(
        [np.ones(4), points, 0.5 * (3.0 * points**2 - 1.0), 0.5 * (5.0 * points**3 - 3.0 * points)],
        axis=1,
    )
    legendre = legendre * np.sqrt((2.0 * np.arange(4) + 1.0) / 2.0)
    gram = np.sum(weights[:, None] * legendre * legendre, axis=0)
    modal_map = (legendre * weights[:, None]).T / gram[:, None]
    return (weights, derivative, modal_map)


def diagonal_of(derivative):
    return [derivative[node_at, node_at] for node_at in range(4)]


def along(values, length, axis_pos, array_rank):
    shape_list = [1] * array_rank
    shape_list[axis_pos] = length
    return jnp.asarray(
        np.tile(np.asarray([float(item) for item in values]), length // 4).reshape(shape_list)
    )


def log_mean(left, right):
    ratio_sq = ((left - right) / (left + right)) ** 2
    is_close = ratio_sq < 0.0001
    series = (left + right) / (
        2.0 + ratio_sq * (2.0 / 3.0 + ratio_sq * (2.0 / 5.0 + ratio_sq * 2.0 / 7.0))
    )
    top_part = jnp.where(is_close, 1.0, right - left)
    low_part = jnp.where(is_close, 1.0, jnp.log(right / left))
    return jnp.where(is_close, series, top_part / low_part)


def describe(conserved, direction):
    density = conserved[0]
    velocity = conserved[1:4] / density
    pressure = (gamma_gas - 1.0) * (conserved[4] - 0.5 * jnp.sum(conserved[1:4] * velocity, axis=0))
    normal_vel = velocity[direction]
    momentum_flux = [
        conserved[1 + comp] * normal_vel + (pressure if comp == direction else 0.0)
        for comp in range(3)
    ]
    energy_flux = (conserved[4] + pressure) * normal_vel
    sound = jnp.sqrt(gamma_gas * pressure / density)
    return jnp.stack(
        [
            conserved[0],
            conserved[1],
            conserved[2],
            conserved[3],
            conserved[4],
            velocity[0],
            velocity[1],
            velocity[2],
            pressure,
            conserved[1 + direction],
        ]
        + momentum_flux
        + [energy_flux, jnp.abs(normal_vel) + sound]
    )


def euler_interface(left, right):
    speed = jnp.maximum(left[14], right[14])
    return 0.5 * (left[9:14] + right[9:14]) - 0.5 * speed * (right[0:5] - left[0:5])


def two_point(left, right, direction):
    rho_mean = log_mean(left[0], right[0])
    inv_mean = left[8] * right[8] / log_mean(left[0] * right[8], right[0] * left[8])
    vel_avg = 0.5 * (left[5:8] + right[5:8])
    pres_avg = 0.5 * (left[8] + right[8])
    vel_product = 0.5 * jnp.sum(left[5:8] * right[5:8], axis=0)
    mass_flux = rho_mean * vel_avg[direction]
    momentum = [
        mass_flux * vel_avg[comp] + (pres_avg if comp == direction else 0.0) for comp in range(3)
    ]
    energy = mass_flux * (vel_product + inv_mean / (gamma_gas - 1.0)) + 0.5 * (
        left[8] * right[5 + direction] + right[8] * left[5 + direction]
    )
    return jnp.stack([mass_flux] + momentum + [energy])


def euler_direction(described, low_desc, high_desc, direction):
    weights, derivative, modal_map = lgl_tables()
    axis_pos = direction + 1
    length = described.shape[axis_pos]
    array_rank = described.ndim
    prev_desc = jnp.concatenate(
        [low_desc, lax.slice_in_dim(described, 0, length - 1, axis=axis_pos)], axis=axis_pos
    )
    face_flux = euler_interface(prev_desc, described)
    last_face = euler_interface(
        lax.slice_in_dim(described, length - 1, length, axis=axis_pos), high_desc
    )
    next_faces = jnp.concatenate(
        [lax.slice_in_dim(face_flux, 1, length, axis=axis_pos), last_face], axis=axis_pos
    )
    own_flux = described[9:14]
    volume = (
        along([2.0 * item for item in diagonal_of(derivative)], length, axis_pos, array_rank)
        * own_flux
    )
    for offset in range(1, 4):
        partner = jnp.roll(described, -offset, axis=axis_pos)
        pair_flux = two_point(described, partner, direction)
        upward = [
            2.0 * derivative[node_at, node_at + offset] if node_at + offset < 4 else 0.0
            for node_at in range(4)
        ]
        downward = [
            2.0 * derivative[node_at, node_at - offset] if node_at - offset >= 0 else 0.0
            for node_at in range(4)
        ]
        volume = (
            volume
            + along(upward, length, axis_pos, array_rank) * pair_flux
            + along(downward, length, axis_pos, array_rank)
            * jnp.roll(pair_flux, offset, axis=axis_pos)
        )
    first_coef = along([-1.0 / weights[0], 0.0, 0.0, 0.0], length, axis_pos, array_rank)
    last_coef = along([0.0, 0.0, 0.0, 1.0 / weights[3]], length, axis_pos, array_rank)
    dg_part = volume + first_coef * (face_flux - own_flux) + last_coef * (next_faces - own_flux)
    fv_part = along(1.0 / weights, length, axis_pos, array_rank) * (next_faces - face_flux)
    return (dg_part, fv_part)


def section_rate_from(euler_state, gravity_state, low_states, high_states, alpha):
    dg_total = 0.0
    fv_total = 0.0
    speed_total = 0.0
    for direction in range(3):
        described = describe(euler_state, direction)
        dg_part, fv_part = euler_direction(
            described,
            describe(low_states[direction], direction),
            describe(high_states[direction], direction),
            direction,
        )
        dg_total = dg_total + dg_part
        fv_total = fv_total + fv_part
        speed_total = speed_total + described[14]
    grav_grad = gravity_state[1:4]
    source = jnp.concatenate(
        [
            jnp.zeros_like(euler_state[0:1]),
            -euler_state[0:1] * grav_grad,
            -jnp.sum(euler_state[1:4] * grav_grad, axis=0, keepdims=True),
        ],
        axis=0,
    )
    rate = -(2.0 / elem_width) * ((1.0 - alpha) * dg_total + alpha * fv_total) + source
    return (rate, speed_total)


def gravity_flux(gravity, direction):
    zero_field = jnp.zeros_like(gravity[0])
    parts = [-gravity[1 + direction]]
    for comp in range(3):
        parts.append(-gravity[0] / relax_time if comp == direction else zero_field)
    return jnp.stack(parts)


def gravity_interface(left, right, direction):
    return 0.5 * (
        gravity_flux(left, direction) + gravity_flux(right, direction)
    ) - 0.5 * grav_speed * (right - left)


def gravity_direction(gravity, first_face, end_face, direction):
    weights, derivative, modal_map = lgl_tables()
    axis_pos = direction + 1
    length = gravity.shape[axis_pos]
    array_rank = gravity.ndim
    own_flux = gravity_flux(gravity, direction)
    inner = gravity_interface(jnp.roll(gravity, 1, axis=axis_pos), gravity, direction)
    face_flux = jnp.concatenate(
        [first_face, lax.slice_in_dim(inner, 1, length, axis=axis_pos)], axis=axis_pos
    )
    next_faces = jnp.concatenate(
        [lax.slice_in_dim(face_flux, 1, length, axis=axis_pos), end_face], axis=axis_pos
    )
    volume = along(diagonal_of(derivative), length, axis_pos, array_rank) * own_flux
    for offset in range(1, 4):
        upward = [
            derivative[node_at, node_at + offset] if node_at + offset < 4 else 0.0
            for node_at in range(4)
        ]
        downward = [
            derivative[node_at, node_at - offset] if node_at - offset >= 0 else 0.0
            for node_at in range(4)
        ]
        volume = (
            volume
            + along(upward, length, axis_pos, array_rank)
            * jnp.roll(own_flux, -offset, axis=axis_pos)
            + along(downward, length, axis_pos, array_rank)
            * jnp.roll(own_flux, offset, axis=axis_pos)
        )
    first_coef = along([-1.0 / weights[0], 0.0, 0.0, 0.0], length, axis_pos, array_rank)
    last_coef = along([0.0, 0.0, 0.0, 1.0 / weights[3]], length, axis_pos, array_rank)
    return volume + first_coef * (face_flux - own_flux) + last_coef * (next_faces - own_flux)


def gravity_rate(gravity, first_faces, end_faces, density, density_mean):
    total = 0.0
    for direction in range(3):
        total = total + gravity_direction(
            gravity, first_faces[direction], end_faces[direction], direction
        )
    rate = -(2.0 / elem_width) * total
    rate_phi = rate[0:1] - coupling * (density[None] - density_mean)
    rate_grad = rate[1:4] - gravity[1:4] / relax_time
    return jnp.concatenate([rate_phi, rate_grad], axis=0)


def node_weights(grid_shape):
    weights, derivative, modal_map = lgl_tables()
    return (
        along(weights, grid_shape[0], 0, 3)
        * along(weights, grid_shape[1], 1, 3)
        * along(weights, grid_shape[2], 2, 3)
    )


def weighted_total(field):
    return jnp.sum(node_weights(field.shape) * field)


def element_alpha(euler_state):
    weights, derivative, modal_map = lgl_tables()
    density = euler_state[0]
    velocity = euler_state[1:4] / density
    pressure = (gamma_gas - 1.0) * (
        euler_state[4] - 0.5 * jnp.sum(euler_state[1:4] * velocity, axis=0)
    )
    product = density * pressure
    size_x, size_y, size_z = product.shape
    modal_arr = jnp.asarray(modal_map)
    along_x = jnp.einsum(
        "ai,xiyz->xayz",
        modal_arr,
        product.reshape(size_x // 4, 4, size_y, size_z),
        precision=lax.Precision.HIGHEST,
    ).reshape(product.shape)
    along_y = jnp.einsum(
        "bj,xyjz->xybz",
        modal_arr,
        along_x.reshape(size_x, size_y // 4, 4, size_z),
        precision=lax.Precision.HIGHEST,
    ).reshape(product.shape)
    block_modal = jnp.asarray(np.kron(np.eye(size_z // 4), modal_map.T))
    coeffs = jnp.dot(along_y, block_modal, precision=lax.Precision.HIGHEST)
    energy = coeffs * coeffs
    low_index = [1.0, 1.0, 1.0, 0.0]
    low_mask = (
        along(low_index, size_x, 0, 3)
        * along(low_index, size_y, 1, 3)
        * along(low_index, size_z, 2, 3)
    )
    stacked = jnp.stack([energy, energy * (1.0 - low_mask)])
    block_adder = jnp.asarray(np.kron(np.eye(size_z // 4), np.ones((4, 1))))
    summed_z = jnp.dot(stacked, block_adder, precision=lax.Precision.HIGHEST)
    block_sums = jnp.sum(
        summed_z.reshape(2, size_x // 4, 4, size_y // 4, 4, size_z // 4), axis=(2, 4)
    )
    high_share = block_sums[1] / block_sums[0]
    alpha = alpha_most / (1.0 + jnp.exp(-indicator_slope * (high_share - indicator_level)))
    return jnp.repeat(jnp.repeat(jnp.repeat(alpha, 4, axis=0), 4, axis=1), 4, axis=2)


def halo_faces(gravity):
    padded = with_halo(gravity, ((GX, 1), ("gy", 2), (GZ, 3)), 1)
    low_planes = [
        padded[:, 0:1, 1:-1, 1:-1],
        padded[:, 1:-1, 0:1, 1:-1],
        padded[:, 1:-1, 1:-1, 0:1],
    ]
    high_planes = [
        padded[:, -1:, 1:-1, 1:-1],
        padded[:, 1:-1, -1:, 1:-1],
        padded[:, 1:-1, 1:-1, -1:],
    ]
    first_faces = []
    end_faces = []
    for direction in range(3):
        length = gravity.shape[direction + 1]
        first_plane = lax.slice_in_dim(gravity, 0, 1, axis=direction + 1)
        last_plane = lax.slice_in_dim(gravity, length - 1, length, axis=direction + 1)
        first_faces.append(gravity_interface(low_planes[direction], first_plane, direction))
        end_faces.append(gravity_interface(last_plane, high_planes[direction], direction))
    return (first_faces, end_faces)


def local(euler_state, gravity_state):
    grid_shape = euler_state.shape[1:]
    weight_total = (
        8.0
        * (grid_shape[0] // 4)
        * (grid_shape[1] // 4)
        * (grid_shape[2] // 4)
        * lax.axis_size(GX)
        * lax.axis_size("gy")
        * lax.axis_size(GZ)
    )
    early_total = by_axis(weighted_total(euler_state[0]), GX_GY_GZ)
    padded = with_halo(euler_state, ((GX, 1), ("gy", 2), (GZ, 3)), 1)
    low_states = [
        padded[:, 0:1, 1:-1, 1:-1],
        padded[:, 1:-1, 0:1, 1:-1],
        padded[:, 1:-1, 1:-1, 0:1],
    ]
    high_states = [
        padded[:, -1:, 1:-1, 1:-1],
        padded[:, 1:-1, -1:, 1:-1],
        padded[:, 1:-1, 1:-1, -1:],
    ]
    alpha = element_alpha(euler_state)
    rate, speed_total = section_rate_from(
        euler_state, gravity_state, low_states, high_states, alpha
    )
    fastest = over_axes(jnp.max(speed_total), GX_GY_GZ)
    time_step = cfl_euler * elem_width / (7.0 * fastest)
    state_next = euler_state + time_step * rate
    density_mean = early_total / weight_total
    gravity = gravity_state
    rate_grav = jnp.zeros_like(gravity_state)
    for iteration in range(ITERS):
        first_faces, end_faces = halo_faces(gravity)
        rate_grav = gravity_rate(gravity, first_faces, end_faces, state_next[0], density_mean)
        gravity = gravity + pseudo_step * rate_grav
    squared_total = by_axis(weighted_total(rate_grav[0] * rate_grav[0]), GX_GY_GZ)
    residual_norm = jnp.sqrt(squared_total / weight_total)
    grav_grad = gravity[1:4]
    gravity_source = jnp.concatenate(
        [
            -state_next[0:1] * grav_grad,
            -jnp.sum(state_next[1:4] * grav_grad, axis=0, keepdims=True),
        ],
        axis=0,
    )
    return (rate, gravity, gravity_source, residual_norm)


def solution(mesh):
    torus = Mesh(
        mesh.devices.reshape(4, 2, mesh.shape["gy"], 8, 4), ("gx_0", "gx_1", "gy", "gz_0", "gz_1")
    )
    placed = (P(None, GX, "gy", GZ), P(None, GX, "gy", GZ))
    return jax.shard_map(
        local,
        mesh=torus,
        in_specs=placed,
        out_specs=(P(None, GX, "gy", GZ), P(None, GX, "gy", GZ), P(None, GX, "gy", GZ), P()),
        check_vma=False,
    )
```

profile of v0, /device:TPU:4, one launch (start us, length us, event | category | flops | bytes accessed | tf_op | source)
XLA Modules:
  0.0 418.4 jit_solution(7830644081574769389)
XLA Ops:
  0.6 1.0 fusion.397
  1.7 3.5 collective-permute-start.10
  5.1 14.0 %collective-permute-start.11 = (f32[4,4,8,1]{3,2,1,0:T(8,128)S(1)}, f32[4,4,8,1]{3,2,1,0:T(8,128)S(1)}, u32[]{:S(2)}, u32[]{:S(2)}) collective-permute-start(f32[4,4,8,1]{3,2,1,0:T(8,128)S(1)} %get-tuple-element.362), channel_id=1, source_target_pairs={{1,0},{2,1},{3,2},{4,3},{5,4},{6,5},{7,6},{8,7},{9,8},{10,9},{11,1... | collective-permute-start | bytes 1544 | tf_op jit(solution)/shard_map/ppermute | solution.py:38
  19.2 1.9 collective-permute-start.6
  21.2 18.9 %collective-permute-start.7 = (f32[4,1,8,128]{3,2,1,0:T(8,128)S(1)}, f32[4,1,8,128]{3,2,1,0:T(8,128)S(1)}, u32[]{:S(2)}, u32[]{:S(2)}) collective-permute-start(f32[4,1,8,128]{3,2,1,0:T(8,128)S(1)} %get-tuple-element.406), channel_id=1, source_target_pairs={{128,0},{256,128},{384,256},{512,384},{640,512},{768,640},{896,768... | collective-permute-start | bytes 49160 | tf_op jit(solution)/shard_map/ppermute | solution.py:38
  40.1 3.1 collective-permute-start.8
  43.9 0.8 copy-done.1
  45.7 0.6 broadcast_multiply_fusion.5
  47.7 2.7 collective-permute-start.9
  50.5 2.2 collective-permute-start.5
  52.8 4.0 collective-permute-done.5
  56.8 1.9 collective-permute-start.1
  59.3 4.1 collective-permute-start.3
  63.9 1.6 collective-permute-done.3
  71.2 0.7 multiply_reduce_fusion.3
  74.8 0.6 copy-done.29
  76.5 0.7 fusion.198
  77.2 26.7 %pmax.35 = f32[]{:T(128)} all-reduce(f32[]{:T(128)} %get-tuple-element.29), channel_id=1, replica_groups=mesh['gx_0'=4,'gx_1'=2,'gy'=4,'gz_0'=8,'gz_1'=4] {'gx_0'}, use_global_device_ids=true, to_apply=%region_20.21 | all-reduce | flops 1 | bytes 8 | tf_op jit(solution)/shard_map/pmax | solution.py:55
  103.8 22.4 %psum.70 = f32[]{:T(128)} all-reduce(f32[]{:T(128)} %get-tuple-element.28), channel_id=1, replica_groups=mesh['gx_0'=4,'gx_1'=2,'gy'=4,'gz_0'=8,'gz_1'=4] {'gx_0'}, use_global_device_ids=true, to_apply=%region_26.27 | all-reduce | flops 1 | bytes 8 | tf_op jit(solution)/shard_map/psum | solution.py:50
  126.3 3.0 pmax.36
  129.3 3.1 psum.71
  132.4 10.1 %pmax.37 = f32[]{:T(128)} all-reduce(f32[]{:T(128)} %pmax.36), channel_id=1, replica_groups=mesh['gx_0'=4,'gx_1'=2,'gy'=4,'gz_0'=8,'gz_1'=4] {'gy'}, use_global_device_ids=true, to_apply=%region_22.23 | all-reduce | flops 1 | bytes 8 | tf_op jit(solution)/shard_map/pmax | solution.py:55
  142.5 8.7 %psum.72 = f32[]{:T(128)} all-reduce(f32[]{:T(128)} %psum.71), channel_id=1, replica_groups=mesh['gx_0'=4,'gx_1'=2,'gy'=4,'gz_0'=8,'gz_1'=4] {'gy'}, use_global_device_ids=true, to_apply=%region_28.29 | all-reduce | flops 1 | bytes 8 | tf_op jit(solution)/shard_map/psum | solution.py:50
  152.6 25.6 %pmax.38 = f32[]{:T(128)} all-reduce(f32[]{:T(128)} %pmax.37), channel_id=1, replica_groups=mesh['gx_0'=4,'gx_1'=2,'gy'=4,'gz_0'=8,'gz_1'=4] {'gz_0'}, use_global_device_ids=true, to_apply=%region_23.24 | all-reduce | flops 1 | bytes 8 | tf_op jit(solution)/shard_map/pmax | solution.py:55
  178.2 27.7 %psum.73 = f32[]{:T(128)} all-reduce(f32[]{:T(128)} %psum.72), channel_id=1, replica_groups=mesh['gx_0'=4,'gx_1'=2,'gy'=4,'gz_0'=8,'gz_1'=4] {'gz_0'}, use_global_device_ids=true, to_apply=%region_29.30 | all-reduce | flops 1 | bytes 8 | tf_op jit(solution)/shard_map/psum | solution.py:50
  205.9 0.7 copy-done.9
  207.3 2.0 collective-permute-start
  209.3 0.7 fusion.353
  210.1 15.6 %pmax.39 = f32[]{:T(128)} all-reduce(f32[]{:T(128)} %pmax.38), channel_id=1, replica_groups=mesh['gx_0'=4,'gx_1'=2,'gy'=4,'gz_0'=8,'gz_1'=4] {'gz_1'}, use_global_device_ids=true, to_apply=%region_24.25 | all-reduce | flops 1 | bytes 8 | tf_op jit(solution)/shard_map/pmax | solution.py:55
  225.7 8.4 %psum.74 = f32[]{:T(128)} all-reduce(f32[]{:T(128)} %psum.73), channel_id=1, replica_groups=mesh['gx_0'=4,'gx_1'=2,'gy'=4,'gz_0'=8,'gz_1'=4] {'gz_1'}, use_global_device_ids=true, to_apply=%region_30.31 | all-reduce | flops 1 | bytes 8 | tf_op jit(solution)/shard_map/psum | solution.py:50
  234.2 0.6 slice.2182
  235.1 0.7 copy.633
  237.2 0.7 copy-done.14
  238.7 0.7 copy-done.12
  239.5 3.9 collective-permute-start.4
  243.5 0.7 copy-done.8
  244.3 4.2 %collective-permute-start.2 = (f32[5,4,1,128]{3,2,1,0:T(1,128)S(1)}, f32[5,4,1,128]{3,2,1,0:T(1,128)S(1)}, u32[]{:S(2)}, u32[]{:S(2)}) collective-permute-start(f32[5,4,1,128]{3,2,1,0:T(1,128)S(1)} %get-tuple-element.191), channel_id=1, source_target_pairs={{0,32},{32,64},{64,96},{96,0},{1,33},{33,65},{65,97},{97,1},{2,34}... | collective-permute-start | bytes 30728 | tf_op jit(solution)/shard_map/ppermute | solution.py:37
  248.4 6.9 %collective-permute-done.4 = f32[5,4,8,1]{3,2,1,0:T(8,128)S(1)} collective-permute-done((f32[5,4,8,1]{3,2,1,0:T(8,128)S(1)}, f32[5,4,8,1]{3,2,1,0:T(8,128)S(1)}, u32[]{:S(2)}, u32[]{:S(2)}) %collective-permute-start.4) | collective-permute-done | bytes 672 | tf_op jit(solution)/shard_map/ppermute | solution.py:37
  256.0 0.7 copy-done.4
  257.0 0.6 copy-done.11
  257.6 0.7 copy-done.16
  259.7 1.1 multiply_add_fusion
  261.7 4.6 %collective-permute-start.17 = (f32[4,4,8,1]{3,2,1,0:T(8,128)S(1)}, f32[4,4,8,1]{3,2,1,0:T(8,128)S(1)}, u32[]{:S(2)}, u32[]{:S(2)}) collective-permute-start(f32[4,4,8,1]{3,2,1,0:T(8,128)S(1)} %get-tuple-element.300), channel_id=1, source_target_pairs={{1,0},{2,1},{3,2},{4,3},{5,4},{6,5},{7,6},{8,7},{9,8},{10,9},{11,1... | collective-permute-start | bytes 1544 | tf_op jit(solution)/shard_map/ppermute | solution.py:38
  266.3 1.9 collective-permute-start.16
  268.3 4.1 collective-permute-start.15
  272.4 1.9 collective-permute-start.14
  274.3 1.9 collective-permute-start.12
  276.5 12.4 %collective-permute-start.13 = (f32[4,1,8,128]{3,2,1,0:T(8,128)S(1)}, f32[4,1,8,128]{3,2,1,0:T(8,128)S(1)}, u32[]{:S(2)}, u32[]{:S(2)}) collective-permute-start(f32[4,1,8,128]{3,2,1,0:T(8,128)S(1)} %get-tuple-element.344), channel_id=1, source_target_pairs={{128,0},{256,128},{384,256},{512,384},{640,512},{768,640},{896,768... | collective-permute-start | bytes 49160 | tf_op jit(solution)/shard_map/ppermute | solution.py:38
  289.9 0.6 copy-done.23
  290.6 0.7 copy-done.46
  293.3 12.4 %collective-permute-start.23 = (f32[4,4,8,1]{3,2,1,0:T(8,128)S(1)}, f32[4,4,8,1]{3,2,1,0:T(8,128)S(1)}, u32[]{:S(2)}, u32[]{:S(2)}) collective-permute-start(f32[4,4,8,1]{3,2,1,0:T(8,128)S(1)} %get-tuple-element.239), channel_id=1, source_target_pairs={{1,0},{2,1},{3,2},{4,3},{5,4},{6,5},{7,6},{8,7},{9,8},{10,9},{11,1... | collective-permute-start | bytes 1544 | tf_op jit(solution)/shard_map/ppermute | solution.py:38
  305.8 1.9 collective-permute-start.22
  307.8 3.9 collective-permute-start.21
  311.7 2.5 collective-permute-start.20
  314.3 5.3 %collective-permute-start.18 = (f32[4,1,8,128]{3,2,1,0:T(8,128)S(1)}, f32[4,1,8,128]{3,2,1,0:T(8,128)S(1)}, u32[]{:S(2)}, u32[]{:S(2)}) collective-permute-start(f32[4,1,8,128]{3,2,1,0:T(8,128)S(1)} %get-tuple-element.284), channel_id=1, source_target_pairs={{0,128},{128,256},{256,384},{384,512},{512,640},{640,768},{768,896... | collective-permute-start | bytes 49160 | tf_op jit(solution)/shard_map/ppermute | solution.py:37
  319.8 9.0 %collective-permute-start.19 = (f32[4,1,8,128]{3,2,1,0:T(8,128)S(1)}, f32[4,1,8,128]{3,2,1,0:T(8,128)S(1)}, u32[]{:S(2)}, u32[]{:S(2)}) collective-permute-start(f32[4,1,8,128]{3,2,1,0:T(8,128)S(1)} %get-tuple-element.283), channel_id=1, source_target_pairs={{128,0},{256,128},{384,256},{512,384},{640,512},{768,640},{896,768... | collective-permute-start | bytes 49160 | tf_op jit(solution)/shard_map/ppermute | solution.py:38
  329.0 1.2 collective-permute-done.19
  331.0 0.7 fusion.199
  331.6 20.0 %psum.75 = f32[]{:T(128)} all-reduce(f32[]{:T(128)} %get-tuple-element.41), channel_id=1, replica_groups=mesh['gx_0'=4,'gx_1'=2,'gy'=4,'gz_0'=8,'gz_1'=4] {'gx_0'}, use_global_device_ids=true, to_apply=%region_33.34 | all-reduce | flops 1 | bytes 8 | tf_op jit(solution)/shard_map/psum | solution.py:50
  351.7 7.4 %psum.76 = f32[]{:T(128)} all-reduce(f32[]{:T(128)} %psum.75), channel_id=1, replica_groups=mesh['gx_0'=4,'gx_1'=2,'gy'=4,'gz_0'=8,'gz_1'=4] {'gx_1'}, use_global_device_ids=true, to_apply=%region_34.35 | all-reduce | flops 1 | bytes 8 | tf_op jit(solution)/shard_map/psum | solution.py:50
  359.0 11.0 %psum.77 = f32[]{:T(128)} all-reduce(f32[]{:T(128)} %psum.76), channel_id=1, replica_groups=mesh['gx_0'=4,'gx_1'=2,'gy'=4,'gz_0'=8,'gz_1'=4] {'gy'}, use_global_device_ids=true, to_apply=%region_35.36 | all-reduce | flops 1 | bytes 8 | tf_op jit(solution)/shard_map/psum | solution.py:50
  370.0 25.7 %psum.78 = f32[]{:T(128)} all-reduce(f32[]{:T(128)} %psum.77), channel_id=1, replica_groups=mesh['gx_0'=4,'gx_1'=2,'gy'=4,'gz_0'=8,'gz_1'=4] {'gz_0'}, use_global_device_ids=true, to_apply=%region_36.37 | all-reduce | flops 1 | bytes 8 | tf_op jit(solution)/shard_map/psum | solution.py:50
  396.3 19.6 %psum.79 = f32[]{:T(128)} all-reduce(f32[]{:T(128)} %psum.78), channel_id=1, replica_groups=mesh['gx_0'=4,'gx_1'=2,'gy'=4,'gz_0'=8,'gz_1'=4] {'gz_1'}, use_global_device_ids=true, to_apply=%region_37.38 | all-reduce | flops 1 | bytes 8 | tf_op jit(solution)/shard_map/psum | solution.py:50
  416.6 0.6 pad_maximum_fusion.45
  (534 shorter events, 23.8 us)
Async XLA Ops:
  0.6 18.6 %copy-start = (f32[4,4,8,128]{3,2,1,0:T(8,128)S(1)}, f32[4,4,8,128]{3,2,1,0:T(8,128)}, u32[]{:S(2)}) copy-start(f32[4,4,8,128]{3,2,1,0:T(8,128)} %param.126) | copy-start | bytes 196612
  1.7 46.0 %collective-permute-start.10 = (f32[4,4,8,1]{3,2,1,0:T(8,128)S(1)}, f32[4,4,8,1]{3,2,1,0:T(8,128)S(1)}, u32[]{:S(2)}, u32[]{:S(2)}) collective-permute-start(f32[4,4,8,1]{3,2,1,0:T(8,128)S(1)} %get-tuple-element.363), channel_id=1, source_target_pairs={{0,1},{1,2},{2,3},{3,4},{4,5},{5,6},{6,7},{7,8},{8,9},{9,10},{10,1... | collective-permute-start | bytes 1544 | tf_op jit(solution)/shard_map/ppermute | solution.py:37
  5.1 45.3 %collective-permute-start.11 = (f32[4,4,8,1]{3,2,1,0:T(8,128)S(1)}, f32[4,4,8,1]{3,2,1,0:T(8,128)S(1)}, u32[]{:S(2)}, u32[]{:S(2)}) collective-permute-start(f32[4,4,8,1]{3,2,1,0:T(8,128)S(1)} %get-tuple-element.362), channel_id=1, source_target_pairs={{1,0},{2,1},{3,2},{4,3},{5,4},{6,5},{7,6},{8,7},{9,8},{10,9},{11,1... | collective-permute-start | bytes 1544 | tf_op jit(solution)/shard_map/ppermute | solution.py:38
  19.2 47.0 %collective-permute-start.6 = (f32[4,1,8,128]{3,2,1,0:T(8,128)S(1)}, f32[4,1,8,128]{3,2,1,0:T(8,128)S(1)}, u32[]{:S(2)}, u32[]{:S(2)}) collective-permute-start(f32[4,1,8,128]{3,2,1,0:T(8,128)S(1)} %get-tuple-element.407), channel_id=1, source_target_pairs={{0,128},{128,256},{256,384},{384,512},{512,640},{640,768},{768,896... | collective-permute-start | bytes 49160 | tf_op jit(solution)/shard_map/ppermute | solution.py:37
  21.2 45.1 %collective-permute-start.7 = (f32[4,1,8,128]{3,2,1,0:T(8,128)S(1)}, f32[4,1,8,128]{3,2,1,0:T(8,128)S(1)}, u32[]{:S(2)}, u32[]{:S(2)}) collective-permute-start(f32[4,1,8,128]{3,2,1,0:T(8,128)S(1)} %get-tuple-element.406), channel_id=1, source_target_pairs={{128,0},{256,128},{384,256},{512,384},{640,512},{768,640},{896,768... | collective-permute-start | bytes 49160 | tf_op jit(solution)/shard_map/ppermute | solution.py:38
  40.1 19.2 %collective-permute-start.8 = (f32[4,4,1,128]{3,2,1,0:T(1,128)S(1)}, f32[4,4,1,128]{3,2,1,0:T(1,128)S(1)}, u32[]{:S(2)}, u32[]{:S(2)}) collective-permute-start(f32[4,4,1,128]{3,2,1,0:T(1,128)S(1)} %get-tuple-element.392), channel_id=1, source_target_pairs={{0,32},{32,64},{64,96},{96,0},{1,33},{33,65},{65,97},{97,1},{2,34}... | collective-permute-start | bytes 24584 | tf_op jit(solution)/shard_map/ppermute | solution.py:37
  43.8 0.9 copy-start.1
  47.1 5.6 %copy-start.47 = (f32[4]{0:T(128)}, f32[4]{0:T(128)S(1)}, u32[]{:S(2)}) copy-start(f32[4]{0:T(128)S(1)} %get-tuple-element.475) | copy-start | bytes 52
  47.1 19.8 %copy-start.45 = (f32[4]{0:T(128)}, f32[4]{0:T(128)S(1)}, u32[]{:S(2)}) copy-start(f32[4]{0:T(128)S(1)} %get-tuple-element.476) | copy-start | bytes 52
  47.7 15.7 %collective-permute-start.9 = (f32[4,4,1,128]{3,2,1,0:T(1,128)S(1)}, f32[4,4,1,128]{3,2,1,0:T(1,128)S(1)}, u32[]{:S(2)}, u32[]{:S(2)}) collective-permute-start(f32[4,4,1,128]{3,2,1,0:T(1,128)S(1)} %get-tuple-element.391), channel_id=1, source_target_pairs={{32,0},{64,32},{96,64},{0,96},{33,1},{65,33},{97,65},{1,97},{34,2}... | collective-permute-start | bytes 24584 | tf_op jit(solution)/shard_map/ppermute | solution.py:38
  50.5 6.3 %collective-permute-start.5 = (f32[5,4,8,1]{3,2,1,0:T(8,128)S(1)}, f32[5,4,8,1]{3,2,1,0:T(8,128)S(1)}, u32[]{:S(2)}, u32[]{:S(2)}) collective-permute-start(f32[5,4,8,1]{3,2,1,0:T(8,128)S(1)} %bitcast.207), channel_id=1, source_target_pairs={{1,0},{2,1},{3,2},{4,3},{5,4},{6,5},{7,6},{8,7},{9,8},{10,9},{11,1... | collective-permute-start | bytes 1928 | tf_op jit(solution)/shard_map/ppermute | solution.py:38
  56.8 149.1 %collective-permute-start.1 = (f32[5,1,8,128]{3,2,1,0:T(8,128)}, f32[5,1,8,128]{3,2,1,0:T(8,128)S(1)}, u32[]{:S(2)}, u32[]{:S(2)}) collective-permute-start(f32[5,1,8,128]{3,2,1,0:T(8,128)} %slice.1762), channel_id=1, source_target_pairs={{128,0},{256,128},{384,256},{512,384},{640,512},{768,640},{896,768... | collective-permute-start | bytes 61448 | tf_op jit(solution)/shard_map/ppermute | solution.py:38
  59.2 7.0 %copy-start.5 = (f32[5,4,8,1]{3,2,1,0:T(8,128)}, f32[5,4,8,1]{3,2,1,0:T(8,128)S(1)}, u32[]{:S(2)}) copy-start(f32[5,4,8,1]{3,2,1,0:T(8,128)S(1)} %constant_dynamic-update-slice_fusion.125) | copy-start | bytes 1924
  59.3 6.3 %collective-permute-start.3 = (f32[5,4,1,128]{3,2,1,0:T(1,128)S(1)}, f32[5,4,1,128]{3,2,1,0:T(1,128)S(1)}, u32[]{:S(2)}, u32[]{:S(2)}) collective-permute-start(f32[5,4,1,128]{3,2,1,0:T(1,128)S(1)} %slice.1819), channel_id=1, source_target_pairs={{32,0},{64,32},{96,64},{0,96},{33,1},{65,33},{97,65},{1,97},{34,2}... | collective-permute-start | bytes 30728 | tf_op jit(solution)/shard_map/ppermute | solution.py:38
  65.6 143.7 %copy-start.7 = (f32[5,4,1,128]{3,2,1,0:T(1,128)}, f32[5,4,1,128]{3,2,1,0:T(1,128)S(1)}, u32[]{:S(2)}) copy-start(f32[5,4,1,128]{3,2,1,0:T(1,128)S(1)} %collective-permute-done.3) | copy-start | bytes 30724
  67.2 0.7 copy-start.89
  67.2 0.7 copy-start.33
  67.2 0.7 copy-start.35
  67.2 0.7 copy-start.37
  70.4 80.8 %copy-start.3 = (f32[1,4,8,128]{3,2,1,0:T(8,128)}, f32[1,4,8,128]{3,2,1,0:T(8,128)S(1)}, u32[]{:S(2)}) copy-start(f32[1,4,8,128]{3,2,1,0:T(8,128)S(1)} %get-tuple-element.415) | copy-start | bytes 49156
  73.1 0.8 copy-start.93
  73.2 0.9 copy-start.19
  76.5 49.7 %copy-start.15 = (f32[4,8,128]{2,1,0:T(8,128)S(1)}, f32[4,8,128]{2,1,0:T(8,128)}, u32[]{:S(2)}) copy-start(f32[4,8,128]{2,1,0:T(8,128)} %get-tuple-element.37) | copy-start | bytes 49156
  126.3 25.0 %copy-start.6 = (f32[5,4,8,1]{3,2,1,0:T(8,128)S(1)}, f32[5,4,8,1]{3,2,1,0:T(8,128)}, u32[]{:S(2)}) copy-start(f32[5,4,8,1]{3,2,1,0:T(8,128)} %copy-done.5) | copy-start | bytes 1924
  206.6 2.7 copy-start.31
  207.3 2.1 copy-start.27
  207.3 29.8 %collective-permute-start = (f32[5,1,8,128]{3,2,1,0:T(8,128)S(1)}, f32[5,1,8,128]{3,2,1,0:T(8,128)S(1)}, u32[]{:S(2)}, u32[]{:S(2)}) collective-permute-start(f32[5,1,8,128]{3,2,1,0:T(8,128)S(1)} %get-tuple-element.178), channel_id=1, source_target_pairs={{0,128},{128,256},{256,384},{384,512},{512,640},{640,768},{768,896... | collective-permute-start | bytes 61448 | tf_op jit(solution)/shard_map/ppermute | solution.py:37
  239.5 15.8 %collective-permute-start.4 = (f32[5,4,8,1]{3,2,1,0:T(8,128)S(1)}, f32[5,4,8,1]{3,2,1,0:T(8,128)S(1)}, u32[]{:S(2)}, u32[]{:S(2)}) collective-permute-start(f32[5,4,8,1]{3,2,1,0:T(8,128)S(1)} %get-tuple-element.195), channel_id=1, source_target_pairs={{0,1},{1,2},{2,3},{3,4},{4,5},{5,6},{6,7},{7,8},{8,9},{9,10},{10,1... | collective-permute-start | bytes 1928 | tf_op jit(solution)/shard_map/ppermute | solution.py:37
  244.3 12.5 %collective-permute-start.2 = (f32[5,4,1,128]{3,2,1,0:T(1,128)S(1)}, f32[5,4,1,128]{3,2,1,0:T(1,128)S(1)}, u32[]{:S(2)}, u32[]{:S(2)}) collective-permute-start(f32[5,4,1,128]{3,2,1,0:T(1,128)S(1)} %get-tuple-element.191), channel_id=1, source_target_pairs={{0,32},{32,64},{64,96},{96,0},{1,33},{33,65},{65,97},{97,1},{2,34}... | collective-permute-start | bytes 30728 | tf_op jit(solution)/shard_map/ppermute | solution.py:37
  258.7 0.7 copy-start.119
  258.8 0.7 copy-start.120
  258.8 0.7 copy-start.121
  258.8 0.7 copy-start.122
  258.8 0.7 copy-start.123
  261.7 14.8 %collective-permute-start.17 = (f32[4,4,8,1]{3,2,1,0:T(8,128)S(1)}, f32[4,4,8,1]{3,2,1,0:T(8,128)S(1)}, u32[]{:S(2)}, u32[]{:S(2)}) collective-permute-start(f32[4,4,8,1]{3,2,1,0:T(8,128)S(1)} %get-tuple-element.300), channel_id=1, source_target_pairs={{1,0},{2,1},{3,2},{4,3},{5,4},{6,5},{7,6},{8,7},{9,8},{10,9},{11,1... | collective-permute-start | bytes 1544 | tf_op jit(solution)/shard_map/ppermute | solution.py:38
  266.3 22.6 %collective-permute-start.16 = (f32[4,4,8,1]{3,2,1,0:T(8,128)S(1)}, f32[4,4,8,1]{3,2,1,0:T(8,128)S(1)}, u32[]{:S(2)}, u32[]{:S(2)}) collective-permute-start(f32[4,4,8,1]{3,2,1,0:T(8,128)S(1)} %get-tuple-element.301), channel_id=1, source_target_pairs={{0,1},{1,2},{2,3},{3,4},{4,5},{5,6},{6,7},{7,8},{8,9},{9,10},{10,1... | collective-permute-start | bytes 1544 | tf_op jit(solution)/shard_map/ppermute | solution.py:37
  268.3 21.6 %collective-permute-start.15 = (f32[4,4,1,128]{3,2,1,0:T(1,128)S(1)}, f32[4,4,1,128]{3,2,1,0:T(1,128)S(1)}, u32[]{:S(2)}, u32[]{:S(2)}) collective-permute-start(f32[4,4,1,128]{3,2,1,0:T(1,128)S(1)} %get-tuple-element.329), channel_id=1, source_target_pairs={{32,0},{64,32},{96,64},{0,96},{33,1},{65,33},{97,65},{1,97},{34,2}... | collective-permute-start | bytes 24584 | tf_op jit(solution)/shard_map/ppermute | solution.py:38
  272.4 17.5 %collective-permute-start.14 = (f32[4,4,1,128]{3,2,1,0:T(1,128)S(1)}, f32[4,4,1,128]{3,2,1,0:T(1,128)S(1)}, u32[]{:S(2)}, u32[]{:S(2)}) collective-permute-start(f32[4,4,1,128]{3,2,1,0:T(1,128)S(1)} %get-tuple-element.330), channel_id=1, source_target_pairs={{0,32},{32,64},{64,96},{96,0},{1,33},{33,65},{65,97},{97,1},{2,34}... | collective-permute-start | bytes 24584 | tf_op jit(solution)/shard_map/ppermute | solution.py:37
  274.3 16.3 %collective-permute-start.12 = (f32[4,1,8,128]{3,2,1,0:T(8,128)S(1)}, f32[4,1,8,128]{3,2,1,0:T(8,128)S(1)}, u32[]{:S(2)}, u32[]{:S(2)}) collective-permute-start(f32[4,1,8,128]{3,2,1,0:T(8,128)S(1)} %get-tuple-element.345), channel_id=1, source_target_pairs={{0,128},{128,256},{256,384},{384,512},{512,640},{640,768},{768,896... | collective-permute-start | bytes 49160 | tf_op jit(solution)/shard_map/ppermute | solution.py:37
  276.5 14.0 %collective-permute-start.13 = (f32[4,1,8,128]{3,2,1,0:T(8,128)S(1)}, f32[4,1,8,128]{3,2,1,0:T(8,128)S(1)}, u32[]{:S(2)}, u32[]{:S(2)}) collective-permute-start(f32[4,1,8,128]{3,2,1,0:T(8,128)S(1)} %get-tuple-element.344), channel_id=1, source_target_pairs={{128,0},{256,128},{384,256},{512,384},{640,512},{768,640},{896,768... | collective-permute-start | bytes 49160 | tf_op jit(solution)/shard_map/ppermute | solution.py:38
  289.6 1.8 copy-start.56
  289.6 1.8 copy-start.58
  289.6 1.8 copy-start.60
  289.6 1.9 copy-start.62
  289.6 1.9 copy-start.64
  289.6 1.9 copy-start.66
  289.6 1.9 copy-start.68
  289.6 1.9 copy-start.70
  289.6 1.9 copy-start.72
  289.6 1.8 copy-start.74
  289.6 1.8 copy-start.76
  289.7 1.8 copy-start.78
  289.7 1.8 copy-start.80
  289.7 1.8 copy-start.82
  289.7 1.8 copy-start.84
  289.7 1.8 copy-start.86
  289.7 1.8 copy-start.88
  289.7 1.8 copy-start.90
  293.3 26.5 %collective-permute-start.23 = (f32[4,4,8,1]{3,2,1,0:T(8,128)S(1)}, f32[4,4,8,1]{3,2,1,0:T(8,128)S(1)}, u32[]{:S(2)}, u32[]{:S(2)}) collective-permute-start(f32[4,4,8,1]{3,2,1,0:T(8,128)S(1)} %get-tuple-element.239), channel_id=1, source_target_pairs={{1,0},{2,1},{3,2},{4,3},{5,4},{6,5},{7,6},{8,7},{9,8},{10,9},{11,1... | collective-permute-start | bytes 1544 | tf_op jit(solution)/shard_map/ppermute | solution.py:38
  305.8 23.0 %collective-permute-start.22 = (f32[4,4,8,1]{3,2,1,0:T(8,128)S(1)}, f32[4,4,8,1]{3,2,1,0:T(8,128)S(1)}, u32[]{:S(2)}, u32[]{:S(2)}) collective-permute-start(f32[4,4,8,1]{3,2,1,0:T(8,128)S(1)} %get-tuple-element.240), channel_id=1, source_target_pairs={{0,1},{1,2},{2,3},{3,4},{4,5},{5,6},{6,7},{7,8},{8,9},{9,10},{10,1... | collective-permute-start | bytes 1544 | tf_op jit(solution)/shard_map/ppermute | solution.py:37
  307.8 21.2 %collective-permute-start.21 = (f32[4,4,1,128]{3,2,1,0:T(1,128)S(1)}, f32[4,4,1,128]{3,2,1,0:T(1,128)S(1)}, u32[]{:S(2)}, u32[]{:S(2)}) collective-permute-start(f32[4,4,1,128]{3,2,1,0:T(1,128)S(1)} %get-tuple-element.268), channel_id=1, source_target_pairs={{32,0},{64,32},{96,64},{0,96},{33,1},{65,33},{97,65},{1,97},{34,2}... | collective-permute-start | bytes 24584 | tf_op jit(solution)/shard_map/ppermute | solution.py:38
  311.7 17.3 %collective-permute-start.20 = (f32[4,4,1,128]{3,2,1,0:T(1,128)S(1)}, f32[4,4,1,128]{3,2,1,0:T(1,128)S(1)}, u32[]{:S(2)}, u32[]{:S(2)}) collective-permute-start(f32[4,4,1,128]{3,2,1,0:T(1,128)S(1)} %get-tuple-element.269), channel_id=1, source_target_pairs={{0,32},{32,64},{64,96},{96,0},{1,33},{33,65},{65,97},{97,1},{2,34}... | collective-permute-start | bytes 24584 | tf_op jit(solution)/shard_map/ppermute | solution.py:37
  314.3 16.0 %collective-permute-start.18 = (f32[4,1,8,128]{3,2,1,0:T(8,128)S(1)}, f32[4,1,8,128]{3,2,1,0:T(8,128)S(1)}, u32[]{:S(2)}, u32[]{:S(2)}) collective-permute-start(f32[4,1,8,128]{3,2,1,0:T(8,128)S(1)} %get-tuple-element.284), channel_id=1, source_target_pairs={{0,128},{128,256},{256,384},{384,512},{512,640},{640,768},{768,896... | collective-permute-start | bytes 49160 | tf_op jit(solution)/shard_map/ppermute | solution.py:37
  319.8 10.4 %collective-permute-start.19 = (f32[4,1,8,128]{3,2,1,0:T(8,128)S(1)}, f32[4,1,8,128]{3,2,1,0:T(8,128)S(1)}, u32[]{:S(2)}, u32[]{:S(2)}) collective-permute-start(f32[4,1,8,128]{3,2,1,0:T(8,128)S(1)} %get-tuple-element.283), channel_id=1, source_target_pairs={{128,0},{256,128},{384,256},{512,384},{640,512},{768,640},{896,768... | collective-permute-start | bytes 49160 | tf_op jit(solution)/shard_map/ppermute | solution.py:38
  (84 other events, 57.6 us)
where the time goes:
time: 421 us; the launch traced here: 418 us
  blocking collectives  235 us (56%)
  starting transfers between devices  124 us (29%)
  local copies, waits for them, and re-layouts  22.4 us (5%)
  other arithmetic  15.7 us (4%)
  waiting for transfers between devices  13.8 us (3%)
  between operations  6.6 us (2%)
    psum x10, blocking collectives, by_axis(): return functools.reduce(lax.psum, axes, value)  154 us
    ppermute x12, starting transfers between devices, with_halo(): lax.ppermute(first, axis, [(b, a) for a, b in up])  90.2 us
    pmax x5, blocking collectives, over_axes(): value = lax.pmax(value, axis)  81.1 us
    ppermute x12, starting transfers between devices, with_halo(): lax.ppermute(last, axis, up)  34.1 us
    unnamed x266, local copies, waits for them, and re-layouts  16.1 us
  transfers between devices with their start and end apart: 24, of which 4 were waited for; matrix products, arithmetic and copies ran while one was open for 4% of the time, Pallas kernels for 0%

commit v1 on v0

v1 whole, which is shorter than its diff:
```python
import functools
import math

import jax
import jax.numpy as jnp
import numpy as np
from jax import lax
from jax.experimental import pallas as pl
from jax.experimental.pallas import tpu as pltpu
from jax.sharding import Mesh
from jax.sharding import PartitionSpec as P

ITERS = 3
GX = ("gx_0", "gx_1")
GZ = ("gz_0", "gz_1")

gamma_gas = 1.4
elem_width = 1.0
cfl_euler = 0.5
alpha_most = 0.5
indicator_level = 0.5 * 10.0 ** (-1.8 * 4.0**0.25)
indicator_slope = math.log((1.0 - 0.0001) / 0.0001) / indicator_level
coupling = 10.0
pseudo_step = 0.3 * elem_width / 7.0
rho_offset = 2.3

NX, NY, NZ = (4, 8, 128)
F32 = jnp.float32


def lgl_tables():
    points = np.array([-1.0, -1.0 / math.sqrt(5.0), 1.0 / math.sqrt(5.0), 1.0])
    weights = np.array([1.0, 5.0, 5.0, 1.0]) / 6.0
    barycentric = np.array(
        [1.0 / np.prod([points[a] - points[b] for b in range(4) if b != a]) for a in range(4)]
    )
    derivative = np.zeros((4, 4))
    for a in range(4):
        for b in range(4):
            if b != a:
                derivative[a, b] = barycentric[b] / barycentric[a] / (points[a] - points[b])
        derivative[a, a] = -np.sum(derivative[a])
    legendre = np.stack(
        [np.ones(4), points, 0.5 * (3.0 * points**2 - 1.0), 0.5 * (5.0 * points**3 - 3.0 * points)],
        axis=1,
    )
    legendre = legendre * np.sqrt((2.0 * np.arange(4) + 1.0) / 2.0)
    gram = np.sum(weights[:, None] * legendre * legendre, axis=0)
    modal_map = (legendre * weights[:, None]).T / gram[:, None]
    return (weights, derivative, modal_map)


WEIGHTS, DERIV, MODAL = lgl_tables()


class Line:
    def __init__(self, dim):
        self.dim = dim
        self.length = (NY, NZ)[dim]
        self.at = lax.broadcasted_iota(jnp.int32, (NY, NZ), dim)
        self.node = self.at % 4
        self.lowest = self.at == 0
        self.highest = self.at == self.length - 1
        self.is0 = self.node == 0
        self.is3 = self.node == 3

    def by_node(self, values):
        v = [float(item) for item in values]
        if v[1] == v[2] and v[0] == v[3]:
            return jnp.where(self.is0 | self.is3, v[0], v[1]).astype(F32)
        return jnp.where(
            self.node < 2,
            jnp.where(self.is0, v[0], v[1]),
            jnp.where(self.is3, v[3], v[2]),
        ).astype(F32)

    def roll(self, value, by):
        return pltpu.roll(value, by % self.length, self.dim)

    def cyc(self, value, k):
        return jnp.where(self.node < 4 - k, self.roll(value, -k), self.roll(value, 4 - k))

    def coef(self, matrix, k, scale=1.0):
        return self.by_node([scale * matrix[i, (i + k) % 4] for i in range(4)])

    def element_sum(self, value):
        value = value + self.cyc(value, 2)
        return value + self.cyc(value, 1)


def quad(at):
    return [at[x] for x in range(NX)]


def load(ref):
    return [[ref[c, x] for x in range(NX)] for c in range(ref.shape[0])]


def pack(comps, outs):
    xf, xl, yf, yl, zf, zl = outs
    lane = lax.broadcasted_iota(jnp.int32, (NY, NZ), 1)
    first = jnp.zeros((NY, NZ), F32)
    last = jnp.zeros((NY, NZ), F32)
    for c, comp in enumerate(comps):
        xf[c] = comp[0]
        xl[c] = comp[NX - 1]
        for x in range(NX):
            yf[c, pl.ds(x, 1), :] = comp[x][0:1, :]
            yl[c, pl.ds(x, 1), :] = comp[x][NY - 1 : NY, :]
            k = c * NX + x
            here = lane == k
            first = jnp.where(here, pltpu.roll(comp[x], k, 1) if k else comp[x], first)
            last = jnp.where(here, pltpu.roll(comp[x], k + 1, 1), last)
    zf[...] = first
    zl[...] = last


class Halo:
    def __init__(self, refs):
        self.xlo, self.xhi, self.ylo, self.yhi = refs[:4]
        self.zlo, self.zhi = (refs[4][...], refs[5][...])

    def low(self, dim, c, x):
        if dim == 0:
            return jnp.broadcast_to(self.ylo[c, pl.ds(x, 1), :], (NY, NZ))
        k = c * NX + x
        return pltpu.roll(self.zlo, (NZ - k) % NZ, 1) if k else self.zlo

    def high(self, dim, c, x):
        if dim == 0:
            return jnp.broadcast_to(self.yhi[c, pl.ds(x, 1), :], (NY, NZ))
        k = c * NX + x
        return pltpu.roll(self.zhi, NZ - 1 - k, 1)


def message_shapes(n):
    return [
        jax.ShapeDtypeStruct((n, NY, NZ), F32),
        jax.ShapeDtypeStruct((n, NY, NZ), F32),
        jax.ShapeDtypeStruct((n, NX, NZ), F32),
        jax.ShapeDtypeStruct((n, NX, NZ), F32),
        jax.ShapeDtypeStruct((NY, NZ), F32),
        jax.ShapeDtypeStruct((NY, NZ), F32),
    ]


def log_mean(left, right):
    total = left + right
    gap = right - left
    slope = gap / total
    ratio_sq = slope * slope
    is_close = ratio_sq < 0.0001
    series = 2.0 + ratio_sq * (2.0 / 3.0 + ratio_sq * (2.0 / 5.0 + ratio_sq * (2.0 / 7.0)))
    top = jnp.where(is_close, total, gap)
    low = jnp.where(is_close, series, jnp.log(right / left))
    return top / low


def two_point(left, right, d):
    rho_mean = log_mean(left[0], right[0])
    inv_mean = left[4] * right[4] / log_mean(left[0] * right[4], right[0] * left[4])
    vel = [0.5 * (left[1 + i] + right[1 + i]) for i in range(3)]
    product = left[1] * right[1] + left[2] * right[2] + left[3] * right[3]
    mass = rho_mean * vel[d]
    flux = [mass] + [mass * vel[i] for i in range(3)]
    flux[1 + d] = flux[1 + d] + 0.5 * (left[4] + right[4])
    energy = mass * (0.5 * product + inv_mean * (1.0 / (gamma_gas - 1.0))) + 0.5 * (
        left[4] * right[1 + d] + right[4] * left[1 + d]
    )
    return flux + [energy]


def primitive(u):
    inv = 1.0 / u[0]
    vel = [u[1 + i] * inv for i in range(3)]
    kinetic = u[1] * vel[0] + u[2] * vel[1] + u[3] * vel[2]
    pressure = (gamma_gas - 1.0) * (u[4] - 0.5 * kinetic)
    return (vel, pressure, jnp.sqrt(gamma_gas * pressure * inv))


def face_data(u, d, known=None):
    vel, pressure, sound = known or primitive(u)
    normal = vel[d]
    flux = [u[1 + d]] + [u[1 + i] * normal for i in range(3)] + [(u[4] + pressure) * normal]
    flux[1 + d] = flux[1 + d] + pressure
    return (u, flux, jnp.abs(normal) + sound)


def interface(left, right):
    speed = jnp.maximum(left[2], right[2])
    return [
        0.5 * ((left[1][c] + right[1][c]) - speed * (right[0][c] - left[0][c])) for c in range(5)
    ]


def volume_kernel(u_ref, vol_ref, alpha_ref, fast_ref):
    y, z = (Line(0), Line(1))
    u = load(u_ref)
    known = [primitive([u[c][x] for c in range(5)]) for x in range(NX)]
    nodes = [[u[0][x]] + known[x][0] + [known[x][1]] for x in range(NX)]
    speed = [
        jnp.abs(known[x][0][0]) + jnp.abs(known[x][0][1]) + jnp.abs(known[x][0][2]) + 3.0 * known[x][2]
        for x in range(NX)
    ]
    fast_ref[...] = jnp.maximum(jnp.maximum(speed[0], speed[1]), jnp.maximum(speed[2], speed[3]))

    product = [u[0][x] * known[x][1] for x in range(NX)]
    coeffs = [sum(float(MODAL[a, i]) * product[i] for i in range(4)) for a in range(4)]
    for line in (y, z):
        modal = [line.coef(MODAL, k) for k in range(4)]
        coeffs = [
            modal[0] * value + sum(modal[k] * line.cyc(value, k) for k in range(1, 4))
            for value in coeffs
        ]
    energy = [value * value for value in coeffs]
    total = (energy[0] + energy[1]) + (energy[2] + energy[3])
    low = (energy[0] + energy[1]) + energy[2]
    high = energy[3] + jnp.where(y.is3 | z.is3, low, 0.0)
    share = z.element_sum(y.element_sum(high)) / z.element_sum(y.element_sum(total))
    alpha = alpha_most / (1.0 + jnp.exp(-indicator_slope * (share - indicator_level)))
    alpha_ref[...] = alpha

    volume = [[None] * NX for _ in range(5)]
    for i in range(NX):
        for j in range(i + 1, NX):
            flux = two_point(nodes[i], nodes[j], 0)
            for c in range(5):
                for at, other in ((i, j), (j, i)):
                    term = (2.0 * DERIV[at, other]).astype(np.float32) * flux[c]
                    volume[c][at] = term if volume[c][at] is None else volume[c][at] + term
    for d, line in ((1, y), (2, z)):
        up, across, down = [line.coef(DERIV, k, 2.0) for k in (1, 2, 3)]
        for x in range(NX):
            near = two_point(nodes[x], [line.cyc(a, 1) for a in nodes[x]], d)
            far = two_point(nodes[x], [line.cyc(a, 2) for a in nodes[x]], d)
            for c in range(5):
                volume[c][x] = volume[c][x] + (
                    up * near[c] + down * line.cyc(near[c], 3) + across * far[c]
                )
    keep = 1.0 - alpha
    for c in range(5):
        for x in range(NX):
            vol_ref[c, x] = keep * volume[c][x]


def gravity_parts(field, halo, base, y, z):
    total = [[0.0] * NX for _ in range(4)]
    have = [c for c in range(4) if field[c] is not None]
    where = {c: base + i for i, c in enumerate(have)}

    def diff(c, x):
        return field[c][x]

    for c, partner in ((0, 1), (1, 0)):
        if field[partner] is not None:
            for i in range(NX):
                terms = [float(2.0 * DERIV[i, j]) * field[partner][j] for j in range(NX) if DERIV[i, j] != 0.0]
                total[c][i] = total[c][i] + sum(terms[1:], terms[0])
    jumps = {}
    for c in have:
        jumps[c] = (halo.xlo[where[c]] - field[c][0], halo.xhi[where[c]] - field[c][NX - 1])
        for side, x in ((0, 0), (1, NX - 1)):
            total[c][x] = total[c][x] + 6.0 * jumps[c][side]
    for c, partner in ((0, 1), (1, 0)):
        if partner in jumps:
            total[c][0] = total[c][0] - 6.0 * jumps[partner][0]
            total[c][NX - 1] = total[c][NX - 1] + 6.0 * jumps[partner][1]
    for d, line in ((1, y), (2, z)):
        comp = 1 + d
        diag = line.coef(DERIV, 0, 2.0)
        coefs = [line.coef(DERIV, k, 2.0) for k in range(1, 4)]
        sign = line.by_node([-6.0, 0.0, 0.0, 6.0])
        for x in range(NX):
            for c, partner in ((0, comp), (comp, 0)):
                if field[partner] is not None:
                    value = field[partner][x]
                    term = diag * value
                    for k in range(1, 4):
                        term = term + coefs[k - 1] * line.cyc(value, k)
                    total[c][x] = total[c][x] + term
            gaps = {}
            for c in have:
                value = field[c][x]
                prev = jnp.where(line.lowest, halo.low(line.dim, where[c], x), line.roll(value, 1))
                after = jnp.where(line.highest, halo.high(line.dim, where[c], x), line.roll(value, -1))
                beside = jnp.where(line.is0, prev, jnp.where(line.is3, after, value))
                gaps[c] = beside - value
                total[c][x] = total[c][x] + 6.0 * gaps[c]
            for c, partner in ((0, comp), (comp, 0)):
                if partner in gaps:
                    total[c][x] = total[c][x] + sign * gaps[partner]
    return total


def advance(field, halo, base, y, z, source):
    total = gravity_parts(field, halo, base, y, z)
    phi_rate = [total[0][x] - coupling * source[x] for x in range(NX)]
    new = [[None] * NX for _ in range(4)]
    for x in range(NX):
        change = pseudo_step * phi_rate[x]
        new[0][x] = change if field[0] is None else field[0][x] + change
        for c in range(1, 4):
            if field[c] is None:
                new[c][x] = pseudo_step * total[c][x]
            else:
                new[c][x] = field[c][x] + pseudo_step * (total[c][x] - field[c][x])
    return (new, phi_rate)


def pack_kernel(u_ref, g_ref, *outs):
    pack(load(u_ref) + load(g_ref), outs)


def face_kernel(u_ref, g_ref, vol_ref, alpha_ref, *refs):
    halo = Halo(refs[:6])
    rate_ref, field_ref = refs[6:8]
    outs = refs[8:]
    y, z = (Line(0), Line(1))
    u = load(u_ref)
    g = load(g_ref)
    alpha = alpha_ref[...]
    keep = 1.0 - alpha
    known = [primitive([u[c][x] for c in range(5)]) for x in range(NX)]
    total = load(vol_ref)

    own = [face_data([u[c][x] for c in range(5)], 0, known[x]) for x in range(NX)]
    below = face_data([halo.xlo[c] for c in range(5)], 0)
    above = face_data([halo.xhi[c] for c in range(5)], 0)
    chain = [below] + own + [above]
    faces = [interface(chain[i], chain[i + 1]) for i in range(NX + 1)]
    for x in range(NX):
        inner = alpha * float(1.0 / WEIGHTS[x])
        edge = inner + keep * 6.0
        low_coef = edge if x == 0 else inner
        high_coef = edge if x == NX - 1 else inner
        for c in range(5):
            total[c][x] = total[c][x] + (high_coef * faces[x + 1][c] - low_coef * faces[x][c])
    for d, line in ((1, y), (2, z)):
        inner = alpha * line.by_node(1.0 / WEIGHTS)
        low_coef = inner + keep * line.by_node([6.0, 0.0, 0.0, 0.0])
        high_coef = inner + keep * line.by_node([0.0, 0.0, 0.0, 6.0])
        for x in range(NX):
            mine = face_data([u[c][x] for c in range(5)], d, known[x])
            prev = face_data(
                [
                    jnp.where(line.lowest, halo.low(line.dim, c, x), line.roll(u[c][x], 1))
                    for c in range(5)
                ],
                d,
            )
            after = face_data(
                [jnp.where(line.highest, halo.high(line.dim, c, x), u[c][x]) for c in range(5)], d
            )
            face = interface(prev, mine)
            end = interface(mine, after)
            for c in range(5):
                following = jnp.where(line.highest, end[c], line.roll(face[c], -1))
                total[c][x] = total[c][x] + (high_coef * following - low_coef * face[c])
    rate = [[-2.0 * total[c][x] for x in range(NX)] for c in range(5)]
    for x in range(NX):
        for i in range(3):
            rate[1 + i][x] = rate[1 + i][x] - u[0][x] * g[1 + i][x]
        rate[4][x] = rate[4][x] - (
            u[1][x] * g[1][x] + u[2][x] * g[2][x] + u[3][x] * g[3][x]
        )
        for c in range(5):
            rate_ref[c, x] = rate[c][x]

    source = [u[0][x] - rho_offset for x in range(NX)]
    new, _ = advance(g, halo, 5, y, z, source)
    slope = [(-pseudo_step * coupling) * rate[0][x] for x in range(NX)]
    comps = new + [slope]
    for c in range(5):
        for x in range(NX):
            field_ref[c, x] = comps[c][x]
    pack(comps, outs)


def middle_kernel(u_ref, rate_ref, field_ref, *refs):
    halo = Halo(refs[:6])
    next_ref = refs[6]
    outs = refs[7:]
    y, z = (Line(0), Line(1))
    field = load(field_ref)
    new, _ = advance(field[:4], halo, 0, y, z, [u_ref[0, x] - rho_offset for x in range(NX)])
    slope, _ = advance([field[4], None, None, None], halo, 4, y, z, [rate_ref[0, x] for x in range(NX)])
    comps = new + slope
    for c in range(8):
        for x in range(NX):
            next_ref[c, x] = comps[c][x]
    pack(comps, outs)


def last_kernel(u_ref, rate_ref, field_ref, fast_ref, *refs):
    halo = Halo(refs[:6])
    next_ref, stat_ref = refs[6:]
    y, z = (Line(0), Line(1))
    field = load(field_ref)
    source = [u_ref[0, x] - rho_offset for x in range(NX)]
    new, base_rate = advance(field[:4], halo, 0, y, z, source)
    slope, slope_rate = advance(field[4:], halo, 4, y, z, [rate_ref[0, x] for x in range(NX)])
    comps = new + slope
    for c in range(8):
        for x in range(NX):
            next_ref[c, x] = comps[c][x]
    weight = y.by_node(WEIGHTS) * z.by_node(WEIGHTS)

    def total(values):
        by_x = [float(WEIGHTS[x]) * values[x] for x in range(NX)]
        return jnp.sum(((by_x[0] + by_x[1]) + (by_x[2] + by_x[3])) * weight)

    stats = [
        jnp.max(fast_ref[...]),
        total([a * a for a in base_rate]),
        total([a * b for a, b in zip(base_rate, slope_rate)]),
        total([b * b for b in slope_rate]),
        total(base_rate),
        total(slope_rate),
        total(source),
    ]
    lane = lax.broadcasted_iota(jnp.int32, (1, NZ), 1)
    out = jnp.zeros((1, NZ), F32)
    for i, value in enumerate(stats):
        out = jnp.where(lane == i, value, out)
    stat_ref[...] = out


def finish_kernel(weight_total, u_ref, rate_ref, field_ref, stat_ref, grav_ref, source_ref, norm_ref):
    stat = stat_ref[...]
    part = [stat[:, i : i + 1] for i in range(7)]
    step = cfl_euler * elem_width / (7.0 * part[0])
    mean = part[6] * (1.0 / weight_total)
    shift = coupling * mean
    squares = (
        part[1]
        + step * (2.0 * part[2] + step * part[3])
        + shift * (2.0 * (part[4] + step * part[5]) + shift * weight_total)
    )
    norm_ref[...] = jnp.sqrt(jnp.maximum(squares, 0.0) * (1.0 / weight_total))
    raised = (ITERS * pseudo_step) * shift
    for x in range(NX):
        phi = field_ref[0, x] + step * field_ref[4, x] + raised
        grad = [field_ref[c, x] + step * field_ref[4 + c, x] for c in range(1, 4)]
        grav_ref[0, x] = phi
        for c in range(3):
            grav_ref[1 + c, x] = grad[c]
        rho = u_ref[0, x] + step * rate_ref[0, x]
        work = 0.0
        for c in range(3):
            source_ref[c, x] = -rho * grad[c]
            work = work + (u_ref[1 + c, x] + step * rate_ref[1 + c, x]) * grad[c]
        source_ref[3, x] = -work


def call(kernel, out_shape, flops):
    return pl.pallas_call(
        kernel,
        out_shape=out_shape,
        name=getattr(kernel, "__name__", "finish_kernel"),
        cost_estimate=pl.CostEstimate(flops=flops, bytes_accessed=400000, transcendentals=0),
    )


def exchange(messages):
    received = []
    for axis, first, last in zip((GX, "gy", GZ), messages[0::2], messages[1::2]):
        size = lax.axis_size(axis)
        up = [(i, (i + 1) % size) for i in range(size)]
        received.append(lax.ppermute(last, axis, up))
        received.append(lax.ppermute(first, axis, [(b, a) for a, b in up]))
    return received


def combine(a, b):
    lane = lax.broadcasted_iota(jnp.int32, (1, NZ), 1)
    return jnp.where(lane == 0, jnp.maximum(a, b), a + b)


def swap(stat, axis, mask):
    size = lax.axis_size(axis)
    return combine(stat, lax.ppermute(stat, axis, [(i, i ^ mask) for i in range(size)]))


def slots(stat, axis):
    size = lax.axis_size(axis)
    row = lax.broadcasted_iota(jnp.int32, (size, NZ), 0)
    lane = lax.broadcasted_iota(jnp.int32, (1, NZ), 1)
    every = lax.psum(jnp.where(row == lax.axis_index(axis), stat, 0.0), axis)
    return jnp.where(
        lane == 0, jnp.max(every, axis=0, keepdims=True), jnp.sum(every, axis=0, keepdims=True)
    )


def over_all(stat):
    for axis in ("gx_1", "gy", "gz_1"):
        stat = slots(stat, axis)
    for mask in (1, 2, 4):
        stat = swap(stat, "gz_0", mask)
    return slots(stat, "gx_0")


def shape(*dims):
    return jax.ShapeDtypeStruct(dims, F32)


def local(u, g):
    weight_total = float(
        8.0
        * (u.shape[1] // 4 * lax.axis_size(GX))
        * (u.shape[2] // 4 * lax.axis_size("gy"))
        * (u.shape[3] // 4 * lax.axis_size(GZ))
    )
    full = (NX, NY, NZ)
    messages = call(pack_kernel, message_shapes(9), 10**5)(u, g)
    received = exchange(messages)
    vol, alpha, fast = call(
        volume_kernel, [shape(5, *full), shape(NY, NZ), shape(NY, NZ)], 10**7
    )(u)
    rate, field, *messages = call(
        face_kernel, [shape(5, *full), shape(5, *full)] + message_shapes(5), 10**6
    )(u, g, vol, alpha, *received)
    received = exchange(messages)
    field, *messages = call(middle_kernel, [shape(8, *full)] + message_shapes(8), 10**6)(
        u, rate, field, *received
    )
    received = exchange(messages)
    field, stat = call(last_kernel, [shape(8, *full), shape(1, NZ)], 10**6)(
        u, rate, field, fast, *received
    )
    stat = over_all(stat)
    gravity, gravity_source, norm = call(
        functools.partial(finish_kernel, weight_total),
        [shape(4, *full), shape(4, *full), shape(1, 1)],
        10**5,
    )(u, rate, field, stat)
    return (rate, gravity, gravity_source, norm.reshape(()))


def solution(mesh):
    torus = Mesh(
        mesh.devices.reshape(4, 2, mesh.shape["gy"], 8, 4), ("gx_0", "gx_1", "gy", "gz_0", "gz_1")
    )
    placed = (P(None, GX, "gy", GZ), P(None, GX, "gy", GZ))
    return jax.shard_map(
        local,
        mesh=torus,
        in_specs=placed,
        out_specs=(P(None, GX, "gy", GZ), P(None, GX, "gy", GZ), P(None, GX, "gy", GZ), P()),
        check_vma=False,
    )
```

time: 421 us -> 209 us (0.50)
  the two profiles are of different devices: /device:TPU:4 before, /device:TPU:34 now
where the time goes in v1:
time: 209 us; the launch traced here: 208 us
  starting transfers between devices  128 us (61%)
  blocking collectives  48.7 us (23%)
  waiting for transfers between devices  14.5 us (7%)
  Pallas kernels  11.6 us (6%)
  local copies, waits for them, and re-layouts  2.53 us (1%)
    ppermute x9, starting transfers between devices, exchange(): received.append(lax.ppermute(first, axis, [(b, a) for a, b in up]))  69.1 us
    psum x4, blocking collectives, slots(): every = lax.psum(jnp.where(row == lax.axis_index(axis), stat, 0.0), axis)  48.7 us
    ppermute x3, starting transfers between devices, swap(): lax.ppermute(stat, axis, [(i, i ^ mask) for i in range(size)])  34.9 us
    ppermute x9, starting transfers between devices, exchange(): received.append(lax.ppermute(last, axis, up))  24.5 us
    ppermute x3, waiting for transfers between devices, swap(): lax.ppermute(stat, axis, [(i, i ^ mask) for i in range(size)])  7.48 us
  transfers between devices with their start and end apart: 21, of which 7 were waited for; matrix products, arithmetic and copies ran while one was open for 0% of the time, Pallas kernels for 1%

profile of v1, /device:TPU:34, one launch (start us, length us, event | category | flops | bytes accessed | tf_op | source)
XLA Modules:
  0.0 207.9 jit_solution(10755704130036667555)
XLA Ops:
  0.6 1.6 pack_kernel.1
  2.3 2.0 collective-permute-start
  4.3 21.5 %collective-permute-start.1 = (f32[9,8,128]{2,1,0:T(8,128)}, f32[9,8,128]{2,1,0:T(8,128)S(1)}, u32[]{:S(2)}, u32[]{:S(2)}) collective-permute-start(f32[9,8,128]{2,1,0:T(8,128)} %get-tuple-element.36), channel_id=1, source_target_pairs={{128,0},{256,128},{384,256},{512,384},{640,512},{768,640},{896,768... | collective-permute-start | bytes 110600 | tf_op jit(solution)/shard_map/ppermute | solution.py:470
  25.9 3.4 %collective-permute-start.2 = (f32[9,4,128]{2,1,0:T(4,128)}, f32[9,4,128]{2,1,0:T(4,128)S(1)}, u32[]{:S(2)}, u32[]{:S(2)}) collective-permute-start(f32[9,4,128]{2,1,0:T(4,128)} %get-tuple-element.37), channel_id=1, source_target_pairs={{0,32},{32,64},{64,96},{96,0},{1,33},{33,65},{65,97},{97,1},{2,34}... | collective-permute-start | bytes 55304 | tf_op jit(solution)/shard_map/ppermute | solution.py:469
  29.3 2.4 %collective-permute-start.3 = (f32[9,4,128]{2,1,0:T(4,128)}, f32[9,4,128]{2,1,0:T(4,128)S(1)}, u32[]{:S(2)}, u32[]{:S(2)}) collective-permute-start(f32[9,4,128]{2,1,0:T(4,128)} %get-tuple-element.38), channel_id=1, source_target_pairs={{32,0},{64,32},{96,64},{0,96},{33,1},{65,33},{97,65},{1,97},{34,2}... | collective-permute-start | bytes 55304 | tf_op jit(solution)/shard_map/ppermute | solution.py:470
  31.7 3.5 %collective-permute-start.4 = (f32[8,128]{1,0:T(8,128)S(1)}, f32[8,128]{1,0:T(8,128)S(1)}, u32[]{:S(2)}, u32[]{:S(2)}) collective-permute-start(f32[8,128]{1,0:T(8,128)S(1)} %copy-done.23), channel_id=1, source_target_pairs={{0,1},{1,2},{2,3},{3,4},{4,5},{5,6},{6,7},{7,8},{8,9},{9,10},{10,1... | collective-permute-start | bytes 12296 | tf_op jit(solution)/shard_map/ppermute | solution.py:469
  35.2 4.1 %collective-permute-done.4.refs_4_ = f32[8,128]{1,0:T(8,128)S(1)} collective-permute-done((f32[8,128]{1,0:T(8,128)S(1)}, f32[8,128]{1,0:T(8,128)S(1)}, u32[]{:S(2)}, u32[]{:S(2)}) %collective-permute-start.4) | collective-permute-done | bytes 4128 | tf_op jit(solution)/shard_map/ppermute | solution.py:469
  39.3 3.2 %collective-permute-start.5 = (f32[8,128]{1,0:T(8,128)S(1)}, f32[8,128]{1,0:T(8,128)S(1)}, u32[]{:S(2)}, u32[]{:S(2)}) collective-permute-start(f32[8,128]{1,0:T(8,128)S(1)} %copy-done.22), channel_id=1, source_target_pairs={{1,0},{2,1},{3,2},{4,3},{5,4},{6,5},{7,6},{8,7},{9,8},{10,9},{11,1... | collective-permute-start | bytes 12296 | tf_op jit(solution)/shard_map/ppermute | solution.py:470
  42.6 2.0 volume_kernel.1
  44.6 0.3 collective-permute-done.5.refs_5_
  44.8 0.0 collective-permute-done.2.refs_2_
  44.8 0.0 collective-permute-done.3.refs_3_
  44.9 0.0 copy-start
  44.9 0.0 copy-start.1
  44.9 0.5 copy-done.16
  45.4 0.0 copy-done.6
  45.5 0.0 copy-done
  45.5 0.0 copy-done.1
  45.5 2.1 %face_kernel.1 = (f32[5,4,8,128]{3,2,1,0:T(8,128)}, f32[5,4,8,128]{3,2,1,0:T(8,128)}, f32[5,8,128]{2,1,0:T(8,128)}, f32[5,8,128]{2,1,0:T(8,128)}, f32[5,4,128]{2...) custom-call(f32[5,4,8,128]{3,2,1,0:T(8,128)} %u_ref.11, f32[4,4,8,128]{3,2,1,0:T(8,128)} %g_ref.3, ...), custom_call_target="tpu_custom_call" | custom-call | flops 1000000 | bytes 400000 | tf_op jit(solution)/shard_map/face_kernel/pallas_call | solution.py:519
  47.6 2.5 %collective-permute-start.10 = (f32[8,128]{1,0:T(8,128)}, f32[8,128]{1,0:T(8,128)S(1)}, u32[]{:S(2)}, u32[]{:S(2)}) collective-permute-start(f32[8,128]{1,0:T(8,128)} %get-tuple-element.47), channel_id=1, source_target_pairs={{0,1},{1,2},{2,3},{3,4},{4,5},{5,6},{6,7},{7,8},{8,9},{9,10},{10,1... | collective-permute-start | bytes 12296 | tf_op jit(solution)/shard_map/ppermute | solution.py:469
  50.1 1.9 collective-permute-start.6
  52.0 12.4 %collective-permute-start.7 = (f32[5,8,128]{2,1,0:T(8,128)}, f32[5,8,128]{2,1,0:T(8,128)S(1)}, u32[]{:S(2)}, u32[]{:S(2)}) collective-permute-start(f32[5,8,128]{2,1,0:T(8,128)} %get-tuple-element.44), channel_id=1, source_target_pairs={{128,0},{256,128},{384,256},{512,384},{640,512},{768,640},{896,768... | collective-permute-start | bytes 61448 | tf_op jit(solution)/shard_map/ppermute | solution.py:470
  64.4 3.4 %collective-permute-start.8 = (f32[5,4,128]{2,1,0:T(4,128)}, f32[5,4,128]{2,1,0:T(4,128)S(1)}, u32[]{:S(2)}, u32[]{:S(2)}) collective-permute-start(f32[5,4,128]{2,1,0:T(4,128)} %get-tuple-element.45), channel_id=1, source_target_pairs={{0,32},{32,64},{64,96},{96,0},{1,33},{33,65},{65,97},{97,1},{2,34}... | collective-permute-start | bytes 30728 | tf_op jit(solution)/shard_map/ppermute | solution.py:469
  67.8 2.4 %collective-permute-start.9 = (f32[5,4,128]{2,1,0:T(4,128)S(1)}, f32[5,4,128]{2,1,0:T(4,128)S(1)}, u32[]{:S(2)}, u32[]{:S(2)}) collective-permute-start(f32[5,4,128]{2,1,0:T(4,128)S(1)} %copy-done.19), channel_id=1, source_target_pairs={{32,0},{64,32},{96,64},{0,96},{33,1},{65,33},{97,65},{1,97},{34,2}... | collective-permute-start | bytes 30728 | tf_op jit(solution)/shard_map/ppermute | solution.py:470
  70.3 5.6 %collective-permute-start.11 = (f32[8,128]{1,0:T(8,128)S(1)}, f32[8,128]{1,0:T(8,128)S(1)}, u32[]{:S(2)}, u32[]{:S(2)}) collective-permute-start(f32[8,128]{1,0:T(8,128)S(1)} %copy-done.20), channel_id=1, source_target_pairs={{1,0},{2,1},{3,2},{4,3},{5,4},{6,5},{7,6},{8,7},{9,8},{10,9},{11,1... | collective-permute-start | bytes 12296 | tf_op jit(solution)/shard_map/ppermute | solution.py:470
  76.0 1.3 collective-permute-done.11.refs_5_
  77.3 0.5 copy-done.15
  77.8 0.0 copy-done.10
  77.8 0.0 copy-done.11
  77.9 0.0 copy-done.4
  77.9 0.0 copy-done.5
  77.9 1.9 middle_kernel.1
  79.8 2.5 %collective-permute-start.16 = (f32[8,128]{1,0:T(8,128)}, f32[8,128]{1,0:T(8,128)S(1)}, u32[]{:S(2)}, u32[]{:S(2)}) collective-permute-start(f32[8,128]{1,0:T(8,128)} %get-tuple-element.55), channel_id=1, source_target_pairs={{0,1},{1,2},{2,3},{3,4},{4,5},{5,6},{6,7},{7,8},{8,9},{9,10},{10,1... | collective-permute-start | bytes 12296 | tf_op jit(solution)/shard_map/ppermute | solution.py:469
  82.3 1.9 collective-permute-start.12
  84.2 12.4 %collective-permute-start.13 = (f32[8,8,128]{2,1,0:T(8,128)}, f32[8,8,128]{2,1,0:T(8,128)S(1)}, u32[]{:S(2)}, u32[]{:S(2)}) collective-permute-start(f32[8,8,128]{2,1,0:T(8,128)} %get-tuple-element.52), channel_id=1, source_target_pairs={{128,0},{256,128},{384,256},{512,384},{640,512},{768,640},{896,768... | collective-permute-start | bytes 98312 | tf_op jit(solution)/shard_map/ppermute | solution.py:470
  96.6 3.4 %collective-permute-start.14 = (f32[8,4,128]{2,1,0:T(4,128)}, f32[8,4,128]{2,1,0:T(4,128)S(1)}, u32[]{:S(2)}, u32[]{:S(2)}) collective-permute-start(f32[8,4,128]{2,1,0:T(4,128)} %get-tuple-element.53), channel_id=1, source_target_pairs={{0,32},{32,64},{64,96},{96,0},{1,33},{33,65},{65,97},{97,1},{2,34}... | collective-permute-start | bytes 49160 | tf_op jit(solution)/shard_map/ppermute | solution.py:469
  100.0 3.4 %collective-permute-start.15 = (f32[8,4,128]{2,1,0:T(4,128)}, f32[8,4,128]{2,1,0:T(4,128)S(1)}, u32[]{:S(2)}, u32[]{:S(2)}) collective-permute-start(f32[8,4,128]{2,1,0:T(4,128)} %get-tuple-element.54), channel_id=1, source_target_pairs={{32,0},{64,32},{96,64},{0,96},{33,1},{65,33},{97,65},{1,97},{34,2}... | collective-permute-start | bytes 49160 | tf_op jit(solution)/shard_map/ppermute | solution.py:470
  103.4 5.7 %collective-permute-start.17 = (f32[8,128]{1,0:T(8,128)S(1)}, f32[8,128]{1,0:T(8,128)S(1)}, u32[]{:S(2)}, u32[]{:S(2)}) collective-permute-start(f32[8,128]{1,0:T(8,128)S(1)} %copy-done.21), channel_id=1, source_target_pairs={{1,0},{2,1},{3,2},{4,3},{5,4},{6,5},{7,6},{8,7},{9,8},{10,9},{11,1... | collective-permute-start | bytes 12296 | tf_op jit(solution)/shard_map/ppermute | solution.py:470
  109.2 1.3 collective-permute-done.17.refs_5_
  110.5 0.0 copy-start.2
  110.6 0.0 copy-start.3
  110.6 0.5 copy-done.17
  111.1 0.0 copy-done.8
  111.1 0.0 copy-done.9
  111.1 0.0 copy-done.2
  111.2 0.0 copy-done.3
  111.2 2.1 last_kernel.1
  113.2 0.7 copy-done.18
  113.9 0.1 broadcast_select_fusion.3
  114.0 2.4 %psum.28 = f32[2,128]{1,0:T(2,128)S(1)} all-reduce(f32[2,128]{1,0:T(2,128)S(1)} %broadcast_select_fusion.3), channel_id=1, replica_groups=mesh['gx_0'=4,'gx_1'=2,'gy'=4,'gz_0'=8,'gz_1'=4] {'gx_1'}, use_global_device_ids=true, to_apply=%region_0.1 | all-reduce | flops 256 | bytes 2048 | tf_op jit(solution)/shard_map/psum | solution.py:488
  116.4 0.1 broadcast_select_fusion.2
  116.5 10.9 %psum.29 = f32[4,128]{1,0:T(4,128)S(1)} all-reduce(f32[4,128]{1,0:T(4,128)S(1)} %broadcast_select_fusion.2), channel_id=1, replica_groups=mesh['gx_0'=4,'gx_1'=2,'gy'=4,'gz_0'=8,'gz_1'=4] {'gy'}, use_global_device_ids=true, to_apply=%region_3.4 | all-reduce | flops 512 | bytes 4096 | tf_op jit(solution)/shard_map/psum | solution.py:488
  127.5 0.1 broadcast_select_fusion.1
  127.5 11.6 %psum.30 = f32[4,128]{1,0:T(4,128)S(1)} all-reduce(f32[4,128]{1,0:T(4,128)S(1)} %broadcast_select_fusion.1), channel_id=1, replica_groups=mesh['gx_0'=4,'gx_1'=2,'gy'=4,'gz_0'=8,'gz_1'=4] {'gz_1'}, use_global_device_ids=true, to_apply=%region_6.7 | all-reduce | flops 512 | bytes 4096 | tf_op jit(solution)/shard_map/psum | solution.py:488
  139.2 21.3 %collective-permute-start.18 = (f32[1,128]{1,0:T(1,128)S(1)}, f32[1,128]{1,0:T(1,128)S(1)}, u32[]{:S(2)}, u32[]{:S(2)}) collective-permute-start(f32[1,128]{1,0:T(1,128)S(1)} %bitcast_select_fusion.1), channel_id=1, source_target_pairs={{0,4},{4,0},{8,12},{12,8},{16,20},{20,16},{24,28},{28,24},{1,5},{5... | collective-permute-start | bytes 1544 | tf_op jit(solution)/shard_map/ppermute | solution.py:481
  160.5 1.5 collective-permute-done.18
  162.1 1.9 collective-permute-start.19
  164.0 4.4 %collective-permute-done.19 = f32[1,128]{1,0:T(1,128)S(1)} collective-permute-done((f32[1,128]{1,0:T(1,128)S(1)}, f32[1,128]{1,0:T(1,128)S(1)}, u32[]{:S(2)}, u32[]{:S(2)}) %collective-permute-start.19) | collective-permute-done | bytes 544 | tf_op jit(solution)/shard_map/ppermute | solution.py:481
  168.4 11.6 %collective-permute-start.20 = (f32[1,128]{1,0:T(1,128)S(1)}, f32[1,128]{1,0:T(1,128)S(1)}, u32[]{:S(2)}, u32[]{:S(2)}) collective-permute-start(f32[1,128]{1,0:T(1,128)S(1)} %add_select_fusion), channel_id=1, source_target_pairs={{0,16},{4,20},{8,24},{12,28},{16,0},{20,4},{24,8},{28,12},{1,17},{... | collective-permute-start | bytes 1544 | tf_op jit(solution)/shard_map/ppermute | solution.py:481
  180.1 1.5 collective-permute-done.20
  181.6 0.1 broadcast_select_fusion
  181.7 23.7 %psum.31 = f32[4,128]{1,0:T(4,128)S(1)} all-reduce(f32[4,128]{1,0:T(4,128)S(1)} %broadcast_select_fusion), channel_id=1, replica_groups=mesh['gx_0'=4,'gx_1'=2,'gy'=4,'gz_0'=8,'gz_1'=4] {'gx_0'}, use_global_device_ids=true, to_apply=%region_9.10 | all-reduce | flops 512 | bytes 4096 | tf_op jit(solution)/shard_map/psum | solution.py:488
  205.4 0.6 bitcast_select_fusion.stat_ref
  206.0 1.9 finish_kernel.1
  (55 shorter events, 0.2 us)
Async XLA Ops:
  2.3 29.5 %copy-start.23 = (f32[8,128]{1,0:T(8,128)S(1)}, f32[8,128]{1,0:T(8,128)}, u32[]{:S(2)}) copy-start(f32[8,128]{1,0:T(8,128)} %get-tuple-element.39) | copy-start | bytes 12292
  2.3 42.6 %collective-permute-start = (f32[9,8,128]{2,1,0:T(8,128)}, f32[9,8,128]{2,1,0:T(8,128)S(1)}, u32[]{:S(2)}, u32[]{:S(2)}) collective-permute-start(f32[9,8,128]{2,1,0:T(8,128)} %get-tuple-element.35), channel_id=1, source_target_pairs={{0,128},{128,256},{256,384},{384,512},{512,640},{640,768},{768,896... | collective-permute-start | bytes 110600 | tf_op jit(solution)/shard_map/ppermute | solution.py:469
  4.3 35.0 %copy-start.22 = (f32[8,128]{1,0:T(8,128)S(1)}, f32[8,128]{1,0:T(8,128)}, u32[]{:S(2)}) copy-start(f32[8,128]{1,0:T(8,128)} %get-tuple-element.40) | copy-start | bytes 12292
  4.3 40.6 %collective-permute-start.1 = (f32[9,8,128]{2,1,0:T(8,128)}, f32[9,8,128]{2,1,0:T(8,128)S(1)}, u32[]{:S(2)}, u32[]{:S(2)}) collective-permute-start(f32[9,8,128]{2,1,0:T(8,128)} %get-tuple-element.36), channel_id=1, source_target_pairs={{128,0},{256,128},{384,256},{512,384},{640,512},{768,640},{896,768... | collective-permute-start | bytes 110600 | tf_op jit(solution)/shard_map/ppermute | solution.py:470
  25.9 19.0 %collective-permute-start.2 = (f32[9,4,128]{2,1,0:T(4,128)}, f32[9,4,128]{2,1,0:T(4,128)S(1)}, u32[]{:S(2)}, u32[]{:S(2)}) collective-permute-start(f32[9,4,128]{2,1,0:T(4,128)} %get-tuple-element.37), channel_id=1, source_target_pairs={{0,32},{32,64},{64,96},{96,0},{1,33},{33,65},{65,97},{97,1},{2,34}... | collective-permute-start | bytes 55304 | tf_op jit(solution)/shard_map/ppermute | solution.py:469
  29.3 15.6 %collective-permute-start.3 = (f32[9,4,128]{2,1,0:T(4,128)}, f32[9,4,128]{2,1,0:T(4,128)S(1)}, u32[]{:S(2)}, u32[]{:S(2)}) collective-permute-start(f32[9,4,128]{2,1,0:T(4,128)} %get-tuple-element.38), channel_id=1, source_target_pairs={{32,0},{64,32},{96,64},{0,96},{33,1},{65,33},{97,65},{1,97},{34,2}... | collective-permute-start | bytes 55304 | tf_op jit(solution)/shard_map/ppermute | solution.py:470
  31.7 7.6 %collective-permute-start.4 = (f32[8,128]{1,0:T(8,128)S(1)}, f32[8,128]{1,0:T(8,128)S(1)}, u32[]{:S(2)}, u32[]{:S(2)}) collective-permute-start(f32[8,128]{1,0:T(8,128)S(1)} %copy-done.23), channel_id=1, source_target_pairs={{0,1},{1,2},{2,3},{3,4},{4,5},{5,6},{6,7},{7,8},{8,9},{9,10},{10,1... | collective-permute-start | bytes 12296 | tf_op jit(solution)/shard_map/ppermute | solution.py:469
  39.3 5.2 %copy-start.14 = (f32[8,128]{1,0:T(8,128)}, f32[8,128]{1,0:T(8,128)S(1)}, u32[]{:S(2)}) copy-start(f32[8,128]{1,0:T(8,128)S(1)} %collective-permute-done.4.refs_4_) | copy-start | bytes 12292
  39.3 5.5 %collective-permute-start.5 = (f32[8,128]{1,0:T(8,128)S(1)}, f32[8,128]{1,0:T(8,128)S(1)}, u32[]{:S(2)}, u32[]{:S(2)}) collective-permute-start(f32[8,128]{1,0:T(8,128)S(1)} %copy-done.22), channel_id=1, source_target_pairs={{1,0},{2,1},{3,2},{4,3},{5,4},{6,5},{7,6},{8,7},{9,8},{10,9},{11,1... | collective-permute-start | bytes 12296 | tf_op jit(solution)/shard_map/ppermute | solution.py:470
  44.8 0.6 copy-start.16
  44.8 0.6 copy-start.6
  44.9 0.6 copy-start.7
  44.9 0.6 copy-start
  44.9 0.6 copy-start.1
  47.6 20.2 %copy-start.19 = (f32[5,4,128]{2,1,0:T(4,128)S(1)}, f32[5,4,128]{2,1,0:T(4,128)}, u32[]{:S(2)}) copy-start(f32[5,4,128]{2,1,0:T(4,128)} %get-tuple-element.46) | copy-start | bytes 30724
  47.6 22.7 %collective-permute-start.10 = (f32[8,128]{1,0:T(8,128)}, f32[8,128]{1,0:T(8,128)S(1)}, u32[]{:S(2)}, u32[]{:S(2)}) collective-permute-start(f32[8,128]{1,0:T(8,128)} %get-tuple-element.47), channel_id=1, source_target_pairs={{0,1},{1,2},{2,3},{3,4},{4,5},{5,6},{6,7},{7,8},{8,9},{9,10},{10,1... | collective-permute-start | bytes 12296 | tf_op jit(solution)/shard_map/ppermute | solution.py:469
  50.1 20.2 %copy-start.20 = (f32[8,128]{1,0:T(8,128)S(1)}, f32[8,128]{1,0:T(8,128)}, u32[]{:S(2)}) copy-start(f32[8,128]{1,0:T(8,128)} %get-tuple-element.48) | copy-start | bytes 12292
  50.1 27.1 %collective-permute-start.6 = (f32[5,8,128]{2,1,0:T(8,128)}, f32[5,8,128]{2,1,0:T(8,128)S(1)}, u32[]{:S(2)}, u32[]{:S(2)}) collective-permute-start(f32[5,8,128]{2,1,0:T(8,128)} %get-tuple-element.43), channel_id=1, source_target_pairs={{0,128},{128,256},{256,384},{384,512},{512,640},{640,768},{768,896... | collective-permute-start | bytes 61448 | tf_op jit(solution)/shard_map/ppermute | solution.py:469
  52.0 25.2 %collective-permute-start.7 = (f32[5,8,128]{2,1,0:T(8,128)}, f32[5,8,128]{2,1,0:T(8,128)S(1)}, u32[]{:S(2)}, u32[]{:S(2)}) collective-permute-start(f32[5,8,128]{2,1,0:T(8,128)} %get-tuple-element.44), channel_id=1, source_target_pairs={{128,0},{256,128},{384,256},{512,384},{640,512},{768,640},{896,768... | collective-permute-start | bytes 61448 | tf_op jit(solution)/shard_map/ppermute | solution.py:470
  64.4 12.8 %collective-permute-start.8 = (f32[5,4,128]{2,1,0:T(4,128)}, f32[5,4,128]{2,1,0:T(4,128)S(1)}, u32[]{:S(2)}, u32[]{:S(2)}) collective-permute-start(f32[5,4,128]{2,1,0:T(4,128)} %get-tuple-element.45), channel_id=1, source_target_pairs={{0,32},{32,64},{64,96},{96,0},{1,33},{33,65},{65,97},{97,1},{2,34}... | collective-permute-start | bytes 30728 | tf_op jit(solution)/shard_map/ppermute | solution.py:469
  67.8 9.4 %collective-permute-start.9 = (f32[5,4,128]{2,1,0:T(4,128)S(1)}, f32[5,4,128]{2,1,0:T(4,128)S(1)}, u32[]{:S(2)}, u32[]{:S(2)}) collective-permute-start(f32[5,4,128]{2,1,0:T(4,128)S(1)} %copy-done.19), channel_id=1, source_target_pairs={{32,0},{64,32},{96,64},{0,96},{33,1},{65,33},{97,65},{1,97},{34,2}... | collective-permute-start | bytes 30728 | tf_op jit(solution)/shard_map/ppermute | solution.py:470
  70.3 5.7 %copy-start.12 = (f32[8,128]{1,0:T(8,128)}, f32[8,128]{1,0:T(8,128)S(1)}, u32[]{:S(2)}) copy-start(f32[8,128]{1,0:T(8,128)S(1)} %collective-permute-done.10.refs_4_) | copy-start | bytes 12292
  70.3 6.9 %collective-permute-start.11 = (f32[8,128]{1,0:T(8,128)S(1)}, f32[8,128]{1,0:T(8,128)S(1)}, u32[]{:S(2)}, u32[]{:S(2)}) collective-permute-start(f32[8,128]{1,0:T(8,128)S(1)} %copy-done.20), channel_id=1, source_target_pairs={{1,0},{2,1},{3,2},{4,3},{5,4},{6,5},{7,6},{8,7},{9,8},{10,9},{11,1... | collective-permute-start | bytes 12296 | tf_op jit(solution)/shard_map/ppermute | solution.py:470
  77.2 0.6 copy-start.15
  77.2 0.6 copy-start.10
  77.2 0.6 copy-start.11
  77.3 0.6 copy-start.4
  77.3 0.6 copy-start.5
  79.8 23.6 %collective-permute-start.16 = (f32[8,128]{1,0:T(8,128)}, f32[8,128]{1,0:T(8,128)S(1)}, u32[]{:S(2)}, u32[]{:S(2)}) collective-permute-start(f32[8,128]{1,0:T(8,128)} %get-tuple-element.55), channel_id=1, source_target_pairs={{0,1},{1,2},{2,3},{3,4},{4,5},{5,6},{6,7},{7,8},{8,9},{9,10},{10,1... | collective-permute-start | bytes 12296 | tf_op jit(solution)/shard_map/ppermute | solution.py:469
  82.3 21.1 %copy-start.21 = (f32[8,128]{1,0:T(8,128)S(1)}, f32[8,128]{1,0:T(8,128)}, u32[]{:S(2)}) copy-start(f32[8,128]{1,0:T(8,128)} %get-tuple-element.56) | copy-start | bytes 12292
  82.3 28.2 %collective-permute-start.12 = (f32[8,8,128]{2,1,0:T(8,128)}, f32[8,8,128]{2,1,0:T(8,128)S(1)}, u32[]{:S(2)}, u32[]{:S(2)}) collective-permute-start(f32[8,8,128]{2,1,0:T(8,128)} %get-tuple-element.51), channel_id=1, source_target_pairs={{0,128},{128,256},{256,384},{384,512},{512,640},{640,768},{768,896... | collective-permute-start | bytes 98312 | tf_op jit(solution)/shard_map/ppermute | solution.py:469
  84.2 26.3 %collective-permute-start.13 = (f32[8,8,128]{2,1,0:T(8,128)}, f32[8,8,128]{2,1,0:T(8,128)S(1)}, u32[]{:S(2)}, u32[]{:S(2)}) collective-permute-start(f32[8,8,128]{2,1,0:T(8,128)} %get-tuple-element.52), channel_id=1, source_target_pairs={{128,0},{256,128},{384,256},{512,384},{640,512},{768,640},{896,768... | collective-permute-start | bytes 98312 | tf_op jit(solution)/shard_map/ppermute | solution.py:470
  96.6 13.9 %collective-permute-start.14 = (f32[8,4,128]{2,1,0:T(4,128)}, f32[8,4,128]{2,1,0:T(4,128)S(1)}, u32[]{:S(2)}, u32[]{:S(2)}) collective-permute-start(f32[8,4,128]{2,1,0:T(4,128)} %get-tuple-element.53), channel_id=1, source_target_pairs={{0,32},{32,64},{64,96},{96,0},{1,33},{33,65},{65,97},{97,1},{2,34}... | collective-permute-start | bytes 49160 | tf_op jit(solution)/shard_map/ppermute | solution.py:469
  100.0 10.5 %collective-permute-start.15 = (f32[8,4,128]{2,1,0:T(4,128)}, f32[8,4,128]{2,1,0:T(4,128)S(1)}, u32[]{:S(2)}, u32[]{:S(2)}) collective-permute-start(f32[8,4,128]{2,1,0:T(4,128)} %get-tuple-element.54), channel_id=1, source_target_pairs={{32,0},{64,32},{96,64},{0,96},{33,1},{65,33},{97,65},{1,97},{34,2}... | collective-permute-start | bytes 49160 | tf_op jit(solution)/shard_map/ppermute | solution.py:470
  103.4 7.1 %copy-start.13 = (f32[8,128]{1,0:T(8,128)}, f32[8,128]{1,0:T(8,128)S(1)}, u32[]{:S(2)}) copy-start(f32[8,128]{1,0:T(8,128)S(1)} %collective-permute-done.16.refs_4_) | copy-start | bytes 12292
  103.4 7.1 %collective-permute-start.17 = (f32[8,128]{1,0:T(8,128)S(1)}, f32[8,128]{1,0:T(8,128)S(1)}, u32[]{:S(2)}, u32[]{:S(2)}) collective-permute-start(f32[8,128]{1,0:T(8,128)S(1)} %copy-done.21), channel_id=1, source_target_pairs={{1,0},{2,1},{3,2},{4,3},{5,4},{6,5},{7,6},{8,7},{9,8},{10,9},{11,1... | collective-permute-start | bytes 12296 | tf_op jit(solution)/shard_map/ppermute | solution.py:470
  110.5 0.6 copy-start.17
  110.5 0.6 copy-start.8
  110.5 0.6 copy-start.9
  110.5 0.6 copy-start.2
  110.6 0.6 copy-start.3
  113.2 0.7 copy-start.18
  139.2 22.9 %collective-permute-start.18 = (f32[1,128]{1,0:T(1,128)S(1)}, f32[1,128]{1,0:T(1,128)S(1)}, u32[]{:S(2)}, u32[]{:S(2)}) collective-permute-start(f32[1,128]{1,0:T(1,128)S(1)} %bitcast_select_fusion.1), channel_id=1, source_target_pairs={{0,4},{4,0},{8,12},{12,8},{16,20},{20,16},{24,28},{28,24},{1,5},{5... | collective-permute-start | bytes 1544 | tf_op jit(solution)/shard_map/ppermute | solution.py:481
  162.1 6.3 %collective-permute-start.19 = (f32[1,128]{1,0:T(1,128)S(1)}, f32[1,128]{1,0:T(1,128)S(1)}, u32[]{:S(2)}, u32[]{:S(2)}) collective-permute-start(f32[1,128]{1,0:T(1,128)S(1)} %add_select_fusion.1), channel_id=1, source_target_pairs={{0,8},{4,12},{8,0},{12,4},{16,24},{20,28},{24,16},{28,20},{1,9},{5... | collective-permute-start | bytes 1544 | tf_op jit(solution)/shard_map/ppermute | solution.py:481
  168.4 13.2 %collective-permute-start.20 = (f32[1,128]{1,0:T(1,128)S(1)}, f32[1,128]{1,0:T(1,128)S(1)}, u32[]{:S(2)}, u32[]{:S(2)}) collective-permute-start(f32[1,128]{1,0:T(1,128)S(1)} %add_select_fusion), channel_id=1, source_target_pairs={{0,16},{4,20},{8,24},{12,28},{16,0},{20,4},{24,8},{28,12},{1,17},{... | collective-permute-start | bytes 1544 | tf_op jit(solution)/shard_map/ppermute | solution.py:481
